TPU v7x, 8 devices: a whole 2x2x1 slice. The times are simulated.
8 devices in a mesh: dp: 2 (over z, y), tp: 4 (over x, core).
Axes of the slice: x: 2, y: 2, z: 1, core: 2. Of those that a mesh axis runs over, the one named last changes fastest.
Arguments:
- x_seq: bfloat16 [3, 256, 5120], P(None, 'dp'), parts along dimension 1
- cache_len: int32 [256], P('dp'), parts along dimension 0
- k_cache: bfloat16 [256, 8, 256, 128], P('dp', 'tp'), parts along dimension 0
- v_cache: bfloat16 [256, 8, 256, 128], P('dp', 'tp'), parts along dimension 0
- w_q: bfloat16 [5120, 5120], P(None, 'tp')
- w_k: bfloat16 [5120, 1024], P(None, 'tp')
- w_v: bfloat16 [5120, 1024], P(None, 'tp')
- w_o: bfloat16 [5120, 5120], P('tp')
- w_gate: bfloat16 [5120, 13824], P(None, 'tp')
- w_up: bfloat16 [5120, 13824], P(None, 'tp')
- w_down: bfloat16 [13824, 5120], P('tp')
- g_q: bfloat16 [5120], P('tp')
- g_k: bfloat16 [1024], P('tp')
- g_attn: bfloat16 [5120], replicated
- g_mlp: bfloat16 [5120], replicated
Outputs:
- output 1: bfloat16 [3, 256, 5120], P(None, 'dp'), parts along dimension 1
- output 2: bfloat16 [256, 8, 256, 128], P('dp', 'tp'), parts along dimension 0
- output 3: bfloat16 [256, 8, 256, 128], P('dp', 'tp'), parts along dimension 0
There are 2 independent parts. A program takes and returns all parts, laid end to end along the dimension named above; an argument that names none is the same for every part.
All inputs are finite; a program needn't handle non-finite values.
Results may differ from a plain program's by a relative error of at most 0.0196685.
Values are sent between devices in bfloat16 or wider.
A program may use at most 1 GiB of HBM per device.

v0:
```python
import jax
import jax.numpy as jnp
from jax import lax
from jax.sharding import PartitionSpec as P

ROPE_THETA = 500000.0
NORM_EPS = 1e-6


def rms_factor(sq_sum, full_width):
    return lax.rsqrt(sq_sum / full_width + NORM_EPS)


def rope_tables(positions, head_dim):
    half_dim = head_dim // 2
    inv_freq = ROPE_THETA ** (-(jnp.arange(half_dim, dtype=jnp.float32) * (2.0 / head_dim)))
    angles = positions.astype(jnp.float32)[:, None] * inv_freq[None, :]
    return jnp.cos(angles), jnp.sin(angles)


def apply_rope(head_vals, cos_tab, sin_tab):
    half_dim = head_vals.shape[-1] // 2
    lead_half = head_vals[..., :half_dim]
    tail_half = head_vals[..., half_dim:]
    cos_rows = cos_tab[:, None, :]
    sin_rows = sin_tab[:, None, :]
    return jnp.concatenate([lead_half * cos_rows - tail_half * sin_rows, tail_half * cos_rows + lead_half * sin_rows], axis=-1)


def attend(q_rot, k_old, v_old, lengths, new_keys, new_vals):
    score_scale = q_rot.shape[-1] ** -0.5
    seq_max = k_old.shape[2]
    old_scores = jnp.einsum('bkgd,bksd->bkgs', q_rot, k_old, preferred_element_type=jnp.float32) * score_scale
    old_valid = jnp.arange(seq_max)[None, :] < lengths[:, None]
    old_scores = jnp.where(old_valid[:, None, None, :], old_scores, -jnp.inf)
    new_scores = jnp.einsum('bkgd,bktd->bkgt', q_rot, new_keys, preferred_element_type=jnp.float32) * score_scale
    row_max = jnp.maximum(jnp.max(old_scores, axis=-1, keepdims=True), jnp.max(new_scores, axis=-1, keepdims=True))
    old_exp = jnp.exp(old_scores - row_max)
    new_exp = jnp.exp(new_scores - row_max)
    row_sum = jnp.sum(old_exp, axis=-1, keepdims=True) + jnp.sum(new_exp, axis=-1, keepdims=True)
    mixed_vals = jnp.einsum('bkgs,bksd->bkgd', old_exp.astype(jnp.bfloat16), v_old, preferred_element_type=jnp.float32) + jnp.einsum('bkgt,bktd->bkgd', new_exp.astype(jnp.bfloat16), new_vals, preferred_element_type=jnp.float32)
    return (mixed_vals / row_sum).astype(jnp.bfloat16)


def group_psum(part_val):
    return lax.psum(part_val, 'tp')


def layer_steps(x_seq, cache_len, k_cache, v_cache, w_q, w_k, w_v, w_o, w_gate, w_up, w_down, g_q, g_k, g_attn, g_mlp, q_width, kv_width, group_sum):
    num_steps, n_rows, d_model = x_seq.shape
    kv_loc = k_cache.shape[1]
    head_dim = k_cache.shape[-1]
    q_loc = w_q.shape[1] // head_dim
    group_size = q_loc // kv_loc
    gain_q = g_q.astype(jnp.float32)
    gain_k = g_k.astype(jnp.float32)
    gain_a = g_attn.astype(jnp.float32)
    gain_m = g_mlp.astype(jnp.float32)
    new_keys = []
    new_vals = []
    y_list = []
    for step_idx in range(num_steps):
        x_tok = x_seq[step_idx]
        positions = cache_len + step_idx
        q_raw = jnp.dot(x_tok, w_q, preferred_element_type=jnp.float32).astype(jnp.bfloat16).astype(jnp.float32)
        k_raw = jnp.dot(x_tok, w_k, preferred_element_type=jnp.float32).astype(jnp.bfloat16).astype(jnp.float32)
        v_new = jnp.dot(x_tok, w_v, preferred_element_type=jnp.float32).astype(jnp.bfloat16)
        q_sq = group_sum(jnp.sum(q_raw * q_raw, axis=-1, keepdims=True))
        k_sq = group_sum(jnp.sum(k_raw * k_raw, axis=-1, keepdims=True))
        cos_tab, sin_tab = rope_tables(positions, head_dim)
        q_normed = (q_raw * rms_factor(q_sq, q_width) * gain_q).reshape(n_rows, q_loc, head_dim)
        k_normed = (k_raw * rms_factor(k_sq, kv_width) * gain_k).reshape(n_rows, kv_loc, head_dim)
        q_rot = apply_rope(q_normed, cos_tab, sin_tab).astype(jnp.bfloat16).reshape(n_rows, kv_loc, group_size, head_dim)
        new_keys.append(apply_rope(k_normed, cos_tab, sin_tab).astype(jnp.bfloat16))
        new_vals.append(v_new.reshape(n_rows, kv_loc, head_dim))
        attn_vals = attend(q_rot, k_cache, v_cache, cache_len, jnp.stack(new_keys, axis=2), jnp.stack(new_vals, axis=2))
        attn_part = jnp.dot(attn_vals.reshape(n_rows, q_loc * head_dim), w_o, preferred_element_type=jnp.float32).astype(jnp.bfloat16)
        attn_sum = group_sum(attn_part).astype(jnp.float32)
        hidden = (x_tok.astype(jnp.float32) + attn_sum * rms_factor(jnp.sum(attn_sum * attn_sum, axis=-1, keepdims=True), d_model) * gain_a).astype(jnp.bfloat16)
        gate_pre = jnp.dot(hidden, w_gate, preferred_element_type=jnp.float32)
        up_pre = jnp.dot(hidden, w_up, preferred_element_type=jnp.float32)
        act_loc = (jax.nn.silu(gate_pre) * up_pre).astype(jnp.bfloat16)
        mlp_part = jnp.dot(act_loc, w_down, preferred_element_type=jnp.float32).astype(jnp.bfloat16)
        mlp_sum = group_sum(mlp_part).astype(jnp.float32)
        y_tok = (hidden.astype(jnp.float32) + mlp_sum * rms_factor(jnp.sum(mlp_sum * mlp_sum, axis=-1, keepdims=True), d_model) * gain_m).astype(jnp.bfloat16)
        y_list.append(y_tok)
    offsets = jnp.arange(k_cache.shape[2], dtype=jnp.int32)[None, None, :, None] - cache_len[:, None, None, None]
    k_out = k_cache
    v_out = v_cache
    for step_idx in range(num_steps):
        at_slot = offsets == step_idx
        k_out = jnp.where(at_slot, new_keys[step_idx][:, :, None, :], k_out)
        v_out = jnp.where(at_slot, new_vals[step_idx][:, :, None, :], v_out)
    return jnp.stack(y_list), k_out, v_out


def solution(mesh):
    tp_size = mesh.shape['tp']

    def local_run(x_seq, cache_len, k_cache, v_cache, w_q, w_k, w_v, w_o, w_gate, w_up, w_down, g_q, g_k, g_attn, g_mlp):
        return layer_steps(x_seq, cache_len, k_cache, v_cache, w_q, w_k, w_v, w_o, w_gate, w_up, w_down, g_q, g_k, g_attn, g_mlp, w_q.shape[1] * tp_size, w_k.shape[1] * tp_size, group_psum)

    data_spec = P(None, 'dp', None)
    cache_spec = P('dp', 'tp', None, None)
    col_spec = P(None, 'tp')
    row_spec = P('tp', None)
    arg_specs = (data_spec, P('dp'), cache_spec, cache_spec, col_spec, col_spec, col_spec, row_spec, col_spec, col_spec, row_spec, P('tp'), P('tp'), P(None), P(None))
    out_specs = (data_spec, cache_spec, cache_spec)
    return jax.shard_map(local_run, mesh=mesh, in_specs=arg_specs, out_specs=out_specs, check_vma=False)
```

profile of v0, /device:TPU:0, one launch (start us, length us, event | category | flops | bytes accessed | tf_op | source)
XLA Modules:
  0.0 456.9 jit_solution(434217418557626309)
XLA Ops:
  7.2 2.8 fusion.69
  10.8 3.4 fusion.87
  14.2 3.0 fusion.78
  19.9 2.1 multiply_reduce_fusion.2
  21.9 2.1 multiply_reduce_fusion
  26.1 8.9 %all-reduce = (f32[128,1]{0,1:T(1,128)S(1)}, f32[128,1]{0,1:T(1,128)S(1)}, f32[128,1]{0,1:T(1,128)S(1)}, f32[128,1]{0,1:T(1,128)S(1)}, f32[128,1]{0,1:T(1,128)S(1)}, /*index=5*/f32[128,1]{0,1:T(1,128)S(1)}) all-reduce(f32[128,1]{0,1:T(1,128)S(1)} %bitcast.195, f32[128,1]{0,1:T(1,128)S(1)} %bitcast.194, ...), channel_id=1, replica_groups=mesh['dp'=2,'tp'=4] {'tp'}, use_global_device_ids=true, to_apply=%region_23.24 | all-reduce | flops 768 | bytes 6144 | tf_op jit(solution)/shard_map/psum | solution.py:46
  51.5 11.6 %fusion.30 = (f32[128,2,5]{2,1,0:T(2,128)S(1)}, f32[128,2,5,256]{3,2,1,0:T(8,128)}) fusion(pred[128,256]{1,0:T(8,128)(4,1)S(1)} %get-tuple-element.59, bf16[128,2,256,128]{3,2,1,0:T(8,128)(2,1)} %param.17, bf16[128,2,5,64]{3,2,1,0:T(8,128)(2,1)S(1)} %copy.57, bf16[128,2,5,64]{3,2,1,0:T(8,128)(2,1)S(1)} %copy.56), kind=kOutput, calls=%fused_computation.63 | convolution fusion | flops 85523200 | bytes 18453504 | tf_op jit(solution)/shard_map/bkgd,bksd->bkgs/dot_general | solution.py:33
  63.2 10.6 %fusion.153 = f32[128,2,5,256]{3,2,1,0:T(8,128)S(1)} fusion(bf16[128,2,256,128]{3,2,1,0:T(8,128)(2,1)} %param.17, bf16[128,2,5,64]{3,2,1,0:T(8,128)(2,1)} %copy.75, bf16[128,2,5,64]{3,2,1,0:T(8,128)(2,1)} %copy.74), kind=kOutput, calls=%fused_computation.195 | convolution fusion | flops 84541440 | bytes 18415616 | tf_op jit(solution)/shard_map/bkgd,bksd->bkgs/dot_general | solution.py:33
  73.9 4.1 fusion.174
  78.1 3.8 fusion.173
  82.6 11.0 %fusion.33 = (f32[128,2,5]{2,1,0:T(2,128)}, f32[128,2,5]{2,1,0:T(2,128)}, f32[128,2,5]{2,1,0:T(2,128)}, f32[128,2,5,256]{3,2,1,0:T(8,128)}) fusion(f32[128,2,5,256]{3,2,1,0:T(8,128)} %get-tuple-element.80, f32[128,2,5]{2,1,0:T(2,128)} %multiply_maximum_fusion, pred[128,256]{1,0:T(8,128)(4,1)S(1)} %get-tuple-element.59, f32[128,2,5,256]{3,2,1,0:T(8,128)S(1)} %fusion.153, ...), kind=kOutput, calls=%fused_computation.66 | convolution fusion | flops 87814400 | bytes 21090304 | tf_op jit(solution)/shard_map/bkgd,bksd->bkgs/dot_general | solution.py:33
  95.7 9.3 %fusion.90 = f32[128,2,5,128]{3,2,1,0:T(8,128)} fusion(bf16[128,2,256,128]{3,2,1,0:T(8,128)(2,1)} %param.18, f32[128,2,5,256]{3,2,1,0:T(8,128)S(1)} %fusion.153, f32[128,2,5]{2,1,0:T(2,128)S(1)} %max.24, pred[128,256]{1,0:T(8,128)(4,1)S(1)} %get-tuple-element.59), kind=kOutput, calls=%fused_computation.110 | convolution fusion | flops 85196800 | bytes 18781184 | tf_op jit(solution)/shard_map/bkgs,bksd->bkgd/dot_general | solution.py:41
  105.0 2.5 fusion.35
  107.6 3.5 fusion.92
  113.5 8.4 %fusion.60 = bf16[128,2,5,128]{3,2,1,0:T(8,128)(2,1)} fusion(bf16[128,2,256,128]{3,2,1,0:T(8,128)(2,1)} %param.18, f32[128,2,5,256]{3,2,1,0:T(8,128)S(1)} %copy-done.6, f32[128,2,5]{2,1,0:T(2,128)S(1)} %copy-done.16, pred[128,256]{1,0:T(8,128)(4,1)S(1)} %get-tuple-element.59, f32[128,2,5]{2,1,0:T(2,128)S(1)} %get-tuple-element.30, ...), kind=kOutput, calls=%fused_computation.96 | convolution fusion | flops 85852160 | bytes 18594816 | tf_op jit(solution)/shard_map/bkgs,bksd->bkgd/dot_general | solution.py:41
  124.4 2.2 fusion.62
  127.1 2.1 fusion.61
  129.5 7.9 %convolution_convert_fusion.3 = bf16[128,5120]{1,0:T(8,128)(2,1)} fusion(bf16[128,1280]{0,1:T(8,128)(2,1)S(1)} %bitcast.176, bf16[1280,5120]{1,0:T(8,128)(2,1)} %param.22), kind=kOutput, calls=%fused_computation.5 | convolution fusion | flops 1678376960 | bytes 14745600 | tf_op jit(solution)/shard_map/dot_general | solution.py:77
  137.4 7.9 %convolution_convert_fusion.4 = bf16[128,5120]{1,0:T(8,128)(2,1)} fusion(bf16[128,1280]{0,1:T(8,128)(2,1)S(1)} %bitcast.175, bf16[1280,5120]{1,0:T(8,128)(2,1)} %param.22), kind=kOutput, calls=%fused_computation.6 | convolution fusion | flops 1678376960 | bytes 14745600 | tf_op jit(solution)/shard_map/dot_general | solution.py:77
  145.3 3.1 convolution_convert_fusion.5
  149.8 74.4 %all-reduce.8.cloned.1.call-done = (bf16[128,5120]{1,0:T(8,128)(2,1)}, bf16[128,5120]{1,0:T(8,128)(2,1)}, bf16[128,5120]{1,0:T(8,128)(2,1)}) async-done(((bf16[128,5120]{1,0:T(8,128)(2,1)}, bf16[128,5120]{1,0:T(8,128)(2,1)}, bf16[128,5120]{1,0:T(8,128)(2,1)}), (bf16[128,5120]{1,0:T(8,128)(2,1)}, bf16[128,5120]{1,0:T(8,128)(2,1)}, bf16[128,5120]{1,0:T(8,128)(2,1)})) %all-reduce.8.cloned.1.call-update) | async-done | bytes 3932176 | tf_op jit(solution)/shard_map/psum | solution.py:46
  229.3 4.3 fusion.6
  233.6 14.9 %fusion.175 = f32[128,3456]{1,0:T(8,128)} fusion(bf16[128,5120]{1,0:T(8,128)(2,1)S(1)} %get-tuple-element.20, bf16[5120,3456]{1,0:T(8,128)(2,1)} %param.23), kind=kOutput, calls=%fused_computation.248 | convolution fusion | flops 4529848320 | bytes 38469632 | tf_op jit(solution)/shard_map/dot_general | solution.py:80
  248.6 14.9 %fusion.176 = f32[128,3456]{1,0:T(8,128)} fusion(bf16[128,5120]{1,0:T(8,128)(2,1)S(1)} %get-tuple-element.21, bf16[5120,3456]{1,0:T(8,128)(2,1)} %param.23), kind=kOutput, calls=%fused_computation.249 | convolution fusion | flops 4529848320 | bytes 38469632 | tf_op jit(solution)/shard_map/dot_general | solution.py:80
  263.5 26.9 %convolution_convert_fusion.2 = bf16[128,5120]{1,0:T(8,128)(2,1)} fusion(bf16[3456,5120]{1,0:T(8,128)(2,1)} %param.25, bf16[128,5120]{1,0:T(8,128)(2,1)S(1)} %get-tuple-element.20, bf16[5120,3456]{1,0:T(8,128)(2,1)} %param.24, f32[128,3456]{1,0:T(8,128)} %fusion.175), kind=kOutput, calls=%fused_computation.4 | convolution fusion | flops 9063006208 | bytes 75169792 | tf_op jit(solution)/shard_map/dot_general | solution.py:83
  290.4 27.0 %convolution_convert_fusion.1 = bf16[128,5120]{1,0:T(8,128)(2,1)} fusion(bf16[3456,5120]{1,0:T(8,128)(2,1)} %param.25, bf16[128,5120]{1,0:T(8,128)(2,1)S(1)} %get-tuple-element.21, bf16[5120,3456]{1,0:T(8,128)(2,1)} %param.24, f32[128,3456]{1,0:T(8,128)} %fusion.176), kind=kOutput, calls=%fused_computation.3 | convolution fusion | flops 9063006208 | bytes 75169792 | tf_op jit(solution)/shard_map/dot_general | solution.py:83
  317.4 17.6 %fusion.177 = f32[128,3456]{1,0:T(8,128)} fusion(bf16[128,5120]{1,0:T(8,128)(2,1)} %get-tuple-element.22, bf16[5120,3456]{1,0:T(8,128)(2,1)} %param.23), kind=kOutput, calls=%fused_computation.250 | convolution fusion | flops 4529848320 | bytes 38469632 | tf_op jit(solution)/shard_map/dot_general | solution.py:80
  335.0 27.4 %convolution_convert_fusion = bf16[128,5120]{1,0:T(8,128)(2,1)} fusion(bf16[3456,5120]{1,0:T(8,128)(2,1)} %param.25, bf16[128,5120]{1,0:T(8,128)(2,1)} %get-tuple-element.22, bf16[5120,3456]{1,0:T(8,128)(2,1)} %param.24, f32[128,3456]{1,0:T(8,128)} %fusion.177), kind=kOutput, calls=%fused_computation.2 | convolution fusion | flops 9063006208 | bytes 75169792 | tf_op jit(solution)/shard_map/dot_general | solution.py:83
  363.2 23.0 %select_select_fusion = (bf16[128,2,256,128]{3,2,1,0:T(8,128)(2,1)}, bf16[128,2,256,128]{3,2,1,0:T(8,128)(2,1)}) fusion(bf16[128,2,256,128]{3,2,1,0:T(8,128)(2,1)} %param.18, pred[128,256]{1,0:T(8,128)(4,1)S(1)} %copy-done.35, pred[128,256]{1,0:T(8,128)(4,1)S(1)} %copy-done.36, pred[128,256]{1,0:T(8,128)(4,1)S(1)} %copy-done.34, ...), kind=kLoop, calls=%fused_computation | loop fusion | flops 50331648 | bytes 67600384 | tf_op jit(solution)/shard_map/jit(_where)/select_n | solution.py:93
  386.2 52.0 %all-reduce.6.cloned.1.call-done = (bf16[128,5120]{1,0:T(8,128)(2,1)}, bf16[128,5120]{1,0:T(8,128)(2,1)}, bf16[128,5120]{1,0:T(8,128)(2,1)}) async-done(((bf16[128,5120]{1,0:T(8,128)(2,1)}, bf16[128,5120]{1,0:T(8,128)(2,1)}, bf16[128,5120]{1,0:T(8,128)(2,1)}), (bf16[128,5120]{1,0:T(8,128)(2,1)}, bf16[128,5120]{1,0:T(8,128)(2,1)}, bf16[128,5120]{1,0:T(8,128)(2,1)})) %all-reduce.6.cloned.1.call-update) | async-done | bytes 3932176 | tf_op jit(solution)/shard_map/psum | solution.py:46
  443.5 3.3 fusion.44
  446.7 2.2 pad_maximum_fusion
  (203 shorter events, 43.7 us)
Async XLA Ops:
  7.2 10.8 %copy-start = (bf16[5120,256]{1,0:T(8,128)(2,1)S(1)}, bf16[5120,256]{1,0:T(8,128)(2,1)}, u32[]{:S(2)}) copy-start(bf16[5120,256]{1,0:T(8,128)(2,1)} %param.20) | copy-start | bytes 7864324
  7.2 217.0 %all-reduce.8.cloned.1.call-start = ((), (), s32[]{:S(2)}) async-start(), calls=%async_computation.1 | async-start | bytes 7864320 | tf_op jit(solution)/shard_map/psum | solution.py:46
  10.1 103.2 %copy-start.14 = (bf16[128,2,128]{2,1,0:T(2,128)(2,1)}, bf16[128,2,128]{2,1,0:T(2,128)(2,1)S(1)}, u32[]{:S(2)}) copy-start(bf16[128,2,128]{2,1,0:T(2,128)(2,1)S(1)} %reshape.485) | copy-start | bytes 196612
  10.8 6.5 %copy-start.49 = (s32[128]{0:T(128)S(1)}, s32[128]{0:T(128)}, u32[]{:S(2)}) copy-start(s32[128]{0:T(128)} %param.16) | copy-start | bytes 1540
  14.2 5.7 %copy-start.2 = (bf16[5120,1280]{1,0:T(8,128)(2,1)S(1)}, bf16[5120,1280]{1,0:T(8,128)(2,1)}, u32[]{:S(2)}) copy-start(bf16[5120,1280]{1,0:T(8,128)(2,1)} %param.19) | copy-start | bytes 39321604
  37.0 5.2 %copy-start.21 = (f32[128,256]{1,0:T(8,128)S(1)}, f32[128,256]{1,0:T(8,128)}, u32[]{:S(2)}) copy-start(f32[128,256]{1,0:T(8,128)} %get-tuple-element.49) | copy-start | bytes 393220
  38.8 5.7 %copy-start.23 = (bf16[128,2,64]{0,2,1:T(8,128)(2,1)}, bf16[128,2,64]{0,2,1:T(8,128)(2,1)S(1)}, u32[]{:S(2)}) copy-start(bf16[128,2,64]{0,2,1:T(8,128)(2,1)S(1)} %get-tuple-element.32) | copy-start | bytes 98308
  40.6 6.8 %copy-start.25 = (bf16[128,2,64]{0,2,1:T(8,128)(2,1)}, bf16[128,2,64]{0,2,1:T(8,128)(2,1)S(1)}, u32[]{:S(2)}) copy-start(bf16[128,2,64]{0,2,1:T(8,128)(2,1)S(1)} %get-tuple-element.33) | copy-start | bytes 98308
  40.6 6.8 %copy-start.27 = (bf16[128,2,64]{0,2,1:T(8,128)(2,1)}, bf16[128,2,64]{0,2,1:T(8,128)(2,1)S(1)}, u32[]{:S(2)}) copy-start(bf16[128,2,64]{0,2,1:T(8,128)(2,1)S(1)} %get-tuple-element.34) | copy-start | bytes 98308
  63.2 10.6 %copy-start.10 = (bf16[128,2,5,64]{3,2,1,0:T(8,128)(2,1)S(1)}, bf16[128,2,5,64]{3,2,1,0:T(8,128)(2,1)}, u32[]{:S(2)}) copy-start(bf16[128,2,5,64]{3,2,1,0:T(8,128)(2,1)} %copy.63) | copy-start | bytes 491524
  63.2 10.6 %copy-start.11 = (bf16[128,2,5,64]{3,2,1,0:T(8,128)(2,1)S(1)}, bf16[128,2,5,64]{3,2,1,0:T(8,128)(2,1)}, u32[]{:S(2)}) copy-start(bf16[128,2,5,64]{3,2,1,0:T(8,128)(2,1)} %copy.62) | copy-start | bytes 491524
  82.6 24.9 %slice-start.4 = ((s8[16777216]{0:T(1024)(128)(4,1)}), s8[4194304]{0:T(1024)(128)(4,1)S(1)}, s32[]{:S(2)}) async-start(s8[16777216]{0:T(1024)(128)(4,1)} %bitcast.169), calls=%async_computation.6 | async-start | bytes 8388608
  82.6 24.9 %slice-start.5 = ((s8[16777216]{0:T(1024)(128)(4,1)}), s8[4194304]{0:T(1024)(128)(4,1)S(1)}, s32[]{:S(2)}) async-start(s8[16777216]{0:T(1024)(128)(4,1)} %bitcast.169), calls=%async_computation.7 | async-start | bytes 8388608
  95.7 9.3 %copy-start.7 = (f32[128,2,5,256]{3,2,1,0:T(8,128)S(1)}, f32[128,2,5,256]{3,2,1,0:T(8,128)}, u32[]{:S(2)}) copy-start(f32[128,2,5,256]{3,2,1,0:T(8,128)} %get-tuple-element.81) | copy-start | bytes 3932164
  95.7 11.8 %slice-start.6 = ((s8[16777216]{0:T(1024)(128)(4,1)}), s8[4194304]{0:T(1024)(128)(4,1)S(1)}, s32[]{:S(2)}) async-start(s8[16777216]{0:T(1024)(128)(4,1)} %bitcast.169), calls=%async_computation.8 | async-start | bytes 8388608
  95.7 11.8 %slice-start.7 = ((s8[16777216]{0:T(1024)(128)(4,1)}), s8[4194304]{0:T(1024)(128)(4,1)S(1)}, s32[]{:S(2)}) async-start(s8[16777216]{0:T(1024)(128)(4,1)} %bitcast.169), calls=%async_computation.9 | async-start | bytes 8388608
  107.5 5.7 %copy-start.17 = (f32[128,2,5]{2,1,0:T(2,128)S(1)}, f32[128,2,5]{2,1,0:T(2,128)}, u32[]{:S(2)}) copy-start(f32[128,2,5]{2,1,0:T(2,128)} %get-tuple-element.3) | copy-start | bytes 15364
  107.6 5.9 %copy-start.6 = (f32[128,2,5,256]{3,2,1,0:T(8,128)S(1)}, f32[128,2,5,256]{3,2,1,0:T(8,128)}, u32[]{:S(2)}) copy-start(f32[128,2,5,256]{3,2,1,0:T(8,128)} %get-tuple-element.80) | copy-start | bytes 3932164
  107.6 5.9 %copy-start.16 = (f32[128,2,5]{2,1,0:T(2,128)S(1)}, f32[128,2,5]{2,1,0:T(2,128)}, u32[]{:S(2)}) copy-start(f32[128,2,5]{2,1,0:T(2,128)} %multiply_maximum_fusion) | copy-start | bytes 15364
  113.5 9.8 %copy-start.33 = (f32[128,2,5,2]{2,3,1,0:T(2,128)S(1)}, f32[128,2,5,2]{2,3,1,0:T(2,128)}, u32[]{:S(2)}) copy-start(f32[128,2,5,2]{2,3,1,0:T(2,128)} %get-tuple-element.85) | copy-start | bytes 30724
  113.5 10.3 %copy-start.20 = (f32[128,2,5,3]{2,3,1,0:T(4,128)S(1)}, f32[128,2,5,3]{2,3,1,0:T(4,128)}, u32[]{:S(2)}) copy-start(f32[128,2,5,3]{2,3,1,0:T(4,128)} %get-tuple-element.83) | copy-start | bytes 46084
  113.5 10.8 %copy-start.19 = (f32[128,2,5]{2,1,0:T(2,128)S(1)}, f32[128,2,5]{2,1,0:T(2,128)}, u32[]{:S(2)}) copy-start(f32[128,2,5]{2,1,0:T(2,128)} %get-tuple-element.6) | copy-start | bytes 15364
  129.5 15.7 %slice-start = ((s8[13107200]{0:T(1024)(128)(4,1)}), s8[4194304]{0:T(1024)(128)(4,1)S(1)}, s32[]{:S(2)}) async-start(s8[13107200]{0:T(1024)(128)(4,1)} %bitcast.167), calls=%async_computation.2 | async-start | bytes 8388608
  129.5 15.7 %slice-start.1 = ((s8[13107200]{0:T(1024)(128)(4,1)}), s8[4194304]{0:T(1024)(128)(4,1)S(1)}, s32[]{:S(2)}) async-start(s8[13107200]{0:T(1024)(128)(4,1)} %bitcast.167), calls=%async_computation.3 | async-start | bytes 8388608
  137.4 7.9 %slice-start.2 = ((s8[13107200]{0:T(1024)(128)(4,1)}), s8[4194304]{0:T(1024)(128)(4,1)S(1)}, s32[]{:S(2)}) async-start(s8[13107200]{0:T(1024)(128)(4,1)} %bitcast.167), calls=%async_computation.4 | async-start | bytes 8388608
  137.4 7.9 %slice-start.3 = ((s8[13107200]{0:T(1024)(128)(4,1)}), s8[524288]{0:T(1024)(128)(4,1)S(1)}, s32[]{:S(2)}) async-start(s8[13107200]{0:T(1024)(128)(4,1)} %bitcast.167), calls=%async_computation.5 | async-start | bytes 1048576
  148.4 289.8 %all-reduce.6.cloned.1.call-start = ((), (), s32[]{:S(2)}) async-start(), calls=%async_computation | async-start | bytes 7864320 | tf_op jit(solution)/shard_map/psum | solution.py:46
  224.2 5.2 %copy-start.4 = (bf16[3,128,5120]{2,1,0:T(8,128)(2,1)S(1)}, bf16[3,128,5120]{2,1,0:T(8,128)(2,1)}, u32[]{:S(2)}) copy-start(bf16[3,128,5120]{2,1,0:T(8,128)(2,1)} %param.15) | copy-start | bytes 11796484
  363.2 23.0 %copy-start.47 = (bf16[5120]{0:T(1024)(128)(2,1)S(1)}, bf16[5120]{0:T(1024)(128)(2,1)}, u32[]{:S(2)}) copy-start(bf16[5120]{0:T(1024)(128)(2,1)} %param.29) | copy-start | bytes 30724
  438.3 5.2 %copy-start.5 = (bf16[128,5120]{1,0:T(8,128)(2,1)S(1)}, bf16[128,5120]{1,0:T(8,128)(2,1)}, u32[]{:S(2)}) copy-start(bf16[128,5120]{1,0:T(8,128)(2,1)} %get-tuple-element.22) | copy-start | bytes 3932164
  438.3 5.2 %copy-start.8 = (bf16[128,5120]{1,0:T(8,128)(2,1)S(1)}, bf16[128,5120]{1,0:T(8,128)(2,1)}, u32[]{:S(2)}) copy-start(bf16[128,5120]{1,0:T(8,128)(2,1)} %get-tuple-element.14) | copy-start | bytes 3932164
  438.3 5.2 %copy-start.9 = (bf16[128,5120]{1,0:T(8,128)(2,1)S(1)}, bf16[128,5120]{1,0:T(8,128)(2,1)}, u32[]{:S(2)}) copy-start(bf16[128,5120]{1,0:T(8,128)(2,1)} %get-tuple-element.15) | copy-start | bytes 3932164
  (29 other events, 73.4 us)
Sparse Core Ops, SparseCore 0:
  148.6 75.5 all-reduce.7
  362.6 75.6 all-reduce.5
where the time goes:
time: 464 us; the launch traced here: 457 us
  matrix products  232 us (50%)
  waiting for transfers between devices  126 us (27%)
  other arithmetic  53.8 us (12%)
  local copies, waits for them, and re-layouts  20.6 us (4%)
  between operations  15.2 us (3%)
  blocking collectives  8.9 us (2%)
    psum x2, waiting for transfers between devices, group_psum(): return lax.psum(part_val, 'tp')  126 us
    dot_general x3, matrix products, layer_steps(): jnp.dot(act_loc, w_down, preferred_element_type=jnp.float32)  81.3 us
    dot_general x3, matrix products, layer_steps(): gate_pre = jnp.dot(hidden, w_gate, preferred_element_type=jnp.float32)  47.5 us
    dot_general x3, matrix products, attend(): jnp.einsum('bkgd,bksd->bkgs', q_rot, k_old, preferred_element_type=jnp.fl...  33.3 us
    select_n x1, other arithmetic, layer_steps(): v_out = jnp.where(at_slot, new_vals[step_idx][:, :, None, :], v_out)  23 us
    dot_general x3, matrix products, attend(): jnp.einsum('bkgs,bksd->bkgd', old_exp.astype(jnp.bfloat16), v_old, prefer...  21.1 us
    dot_general x3, matrix products, layer_steps(): jnp.dot(attn_vals.reshape(n_rows, q_loc * head_dim), w_o, preferred_eleme...  18.8 us
    concatenate x16, local copies, waits for them, and re-layouts, apply_rope(): jnp.concatenate([lead_half * cos_rows - tail_half * sin_rows, tail_half *...  10.8 us
  transfers between devices with their start and end apart: 2, of which 2 were waited for; matrix products, arithmetic and copies ran while one was open for 5% of the time, Pallas kernels for 0%

commit v1 on v0

v1 whole, which is shorter than its diff:
```python
import functools
import jax
import jax.numpy as jnp
from jax import lax
from jax.experimental import pallas as pl
from jax.experimental.pallas import tpu as pltpu
from jax.sharding import PartitionSpec as P

ROPE_THETA = 500000.0
NORM_EPS = 1e-6
MESH = pl.DeviceIdType.MESH
F32 = jnp.float32
BF16 = jnp.bfloat16

STEPS = 3
BATCH = 128
ROWS = STEPS * BATCH
D_MODEL = 5120
HEAD = 128
KV_LOC = 2
GROUP = 5
Q_LOC = KV_LOC * GROUP
SEQ = 256
FF_LOC = 3456

ANY = pl.BlockSpec(memory_space=pl.ANY)
VM = pl.BlockSpec(memory_space=pltpu.VMEM)
SM = pl.BlockSpec(memory_space=pltpu.SMEM)


N_QKV = 7


def qkv_kernel(x_hbm, wq_hbm, wk_hbm, wv_hbm, gq_ref, gk_ref, cos_ref, sin_ref,
               q_ref, k_ref, v_ref,
               x_v, w_v, raw, q32, sq_own, sq_recv,
               x_sem, w_sem, send_sem, recv_sem):
    me = lax.axis_index('tp')
    barrier = pltpu.get_barrier_semaphore()
    for d in range(1, 4):
        pl.semaphore_signal(barrier, inc=1, device_id={'tp': (me + d) % 4}, device_id_type=MESH)

    x_copy = pltpu.make_async_copy(x_hbm, x_v, x_sem)
    x_copy.start()
    for i in range(5):
        pltpu.make_async_copy(wq_hbm.at[:, pl.ds(i * 256, 256)], w_v.at[i], w_sem.at[i]).start()
    pltpu.make_async_copy(wk_hbm, w_v.at[5], w_sem.at[5]).start()
    pltpu.make_async_copy(wv_hbm, w_v.at[6], w_sem.at[6]).start()
    x_copy.wait()

    def dot_step(i, _):
        pltpu.make_async_copy(wk_hbm, w_v.at[i], w_sem.at[i]).wait()
        res = jnp.dot(x_v[...], w_v[i], preferred_element_type=F32)
        raw[i] = res.astype(BF16).astype(F32)
        return 0

    lax.fori_loop(0, N_QKV, dot_step, 0)

    for t in range(STEPS):
        rows = pl.ds(t * BATCH, BATCH)
        acc = jnp.zeros((BATCH, HEAD), F32)
        for i in range(5):
            for p in range(2):
                piece = raw[i, rows, p * HEAD:(p + 1) * HEAD]
                acc = acc + piece * piece
        q_row = jnp.sum(jnp.transpose(acc), axis=0, keepdims=True)
        acc = jnp.zeros((BATCH, HEAD), F32)
        for p in range(2):
            piece = raw[5, rows, p * HEAD:(p + 1) * HEAD]
            acc = acc + piece * piece
        k_row = jnp.sum(jnp.transpose(acc), axis=0, keepdims=True)
        sq_own[:, t * BATCH:(t + 1) * BATCH] = jnp.concatenate(
            [jnp.broadcast_to(q_row, (8, BATCH)), jnp.broadcast_to(k_row, (8, BATCH))], axis=0)

    pl.semaphore_wait(barrier, 3)
    copies = []
    for d in range(1, 4):
        cp = pltpu.make_async_remote_copy(
            src_ref=sq_own, dst_ref=sq_recv.at[d - 1], send_sem=send_sem.at[d - 1], recv_sem=recv_sem.at[d - 1],
            device_id={'tp': (me + d) % 4}, device_id_type=MESH)
        cp.start()
        copies.append(cp)
    v_ref[...] = raw[6].astype(BF16)
    zero_rows = jnp.zeros((BATCH, HEAD), F32)
    q32[pl.ds(15, BATCH, stride=32), :] = zero_rows
    q32[pl.ds(31, BATCH, stride=32), :] = zero_rows
    for cp in copies:
        cp.wait()

    q_width = float(Q_LOC * HEAD * 4)
    k_width = float(KV_LOC * HEAD * 4)
    for t in range(STEPS):
        cols = slice(t * BATCH, (t + 1) * BATCH)
        rows = pl.ds(t * BATCH, BATCH)
        tot = sq_own[:, cols] + sq_recv[0, :, cols] + sq_recv[1, :, cols] + sq_recv[2, :, cols]
        q_fac = lax.rsqrt(tot[0:1] / q_width + NORM_EPS)
        k_fac = lax.rsqrt(tot[8:9] / k_width + NORM_EPS)
        q_col = jnp.transpose(jnp.broadcast_to(q_fac, (HEAD, BATCH)))
        k_col = jnp.transpose(jnp.broadcast_to(k_fac, (HEAD, BATCH)))
        cos_t = cos_ref[rows, :]
        sin_t = sin_ref[rows, :]
        for hd in range(Q_LOC):
            val = raw[hd // 2, rows, (hd % 2) * HEAD:(hd % 2 + 1) * HEAD]
            val = val * q_col * gq_ref[:, hd * HEAD:(hd + 1) * HEAD]
            rot = val * cos_t + pltpu.roll(val, HEAD // 2, 1) * sin_t
            row = (hd // GROUP) * 16 + t * GROUP + hd % GROUP
            q32[pl.ds(row, BATCH, stride=32), :] = rot
        for kv in range(KV_LOC):
            val = raw[5, rows, kv * HEAD:(kv + 1) * HEAD]
            val = val * k_col * gk_ref[:, kv * HEAD:(kv + 1) * HEAD]
            rot = val * cos_t + pltpu.roll(val, HEAD // 2, 1) * sin_t
            k_ref[rows, kv * HEAD:(kv + 1) * HEAD] = rot.astype(BF16)

    q_ref[...] = q32[...].astype(BF16)


def run_qkv(x2, w_q, w_k, w_v, gq, gk, cos_t, sin_t):
    return pl.pallas_call(
        qkv_kernel,
        out_shape=(jax.ShapeDtypeStruct((BATCH * 32, HEAD), BF16),
                   jax.ShapeDtypeStruct((ROWS, KV_LOC * HEAD), BF16),
                   jax.ShapeDtypeStruct((ROWS, KV_LOC * HEAD), BF16)),
        in_specs=[ANY, ANY, ANY, ANY, VM, VM, VM, VM],
        out_specs=(VM, VM, VM),
        scratch_shapes=[
            pltpu.VMEM((ROWS, D_MODEL), BF16),
            pltpu.VMEM((N_QKV, D_MODEL, 256), BF16),
            pltpu.VMEM((N_QKV, ROWS, 256), F32),
            pltpu.VMEM((BATCH * 32, HEAD), F32),
            pltpu.VMEM((16, ROWS), F32),
            pltpu.VMEM((3, 16, ROWS), F32),
            pltpu.SemaphoreType.DMA,
            pltpu.SemaphoreType.DMA((N_QKV,)),
            pltpu.SemaphoreType.DMA((3,)),
            pltpu.SemaphoreType.DMA((3,)),
        ],
        compiler_params=pltpu.CompilerParams(collective_id=0, has_side_effects=True, vmem_limit_bytes=48 * 1024 * 1024),
        name='qkv_rope',
    )(x2, w_q, w_k, w_v, gq, gk, cos_t, sin_t)


BBLK = 16
N_BLK = BATCH // BBLK
SLOTS = 4


def attn_kernel(len_ref, q_ref, kn_ref, vn_ref, kc_hbm, vc_hbm,
                o_ref, ko_hbm, vo_hbm,
                kbuf, vbuf, o32, in_sem, out_sem):
    def in_copy(i, s, which):
        src = (kc_hbm, vc_hbm)[which]
        dst = (kbuf, vbuf)[which]
        return pltpu.make_async_copy(src.at[pl.ds(i * BBLK, BBLK)], dst.at[s], in_sem.at[which, s])

    def out_copy(i, s, which):
        dst = (ko_hbm, vo_hbm)[which]
        src = (kbuf, vbuf)[which]
        return pltpu.make_async_copy(src.at[s], dst.at[pl.ds(i * BBLK, BBLK)], out_sem.at[which, s])

    for i in range(2):
        in_copy(i, i, 0).start()
        in_copy(i, i, 1).start()

    scale = HEAD ** -0.5
    row_id = lax.broadcasted_iota(jnp.int32, (32, SEQ), 0)
    col_id = lax.broadcasted_iota(jnp.int32, (32, SEQ), 1)
    sub = row_id - jnp.where(row_id >= 16, 16, 0)
    step_of = jnp.where(sub >= 5, 1, 0) + jnp.where(sub >= 10, 1, 0)
    gap = col_id - step_of
    win_id = lax.broadcasted_iota(jnp.int32, (32, HEAD), 0)

    def block(i, _):
        s = i % SLOTS

        @pl.when(i >= 2)
        def _():
            out_copy(i - 2, (i + 2) % SLOTS, 0).wait()
            out_copy(i - 2, (i + 2) % SLOTS, 1).wait()

        @pl.when(i + 2 < N_BLK)
        def _():
            in_copy(i + 2, (i + 2) % SLOTS, 0).start()
            in_copy(i + 2, (i + 2) % SLOTS, 1).start()

        in_copy(i, s, 0).wait()
        in_copy(i, s, 1).wait()

        news = []
        for src in (kn_ref, vn_ref):
            news.append([src[pl.ds(pl.multiple_of(t * BATCH + i * BBLK, BBLK), BBLK), :].astype(F32) for t in range(STEPS)])
        for bl in range(BBLK):
            ln = len_ref[i * BBLK + bl]
            w0 = jnp.minimum((ln // 16) * 16, SEQ - 32)
            win = pl.ds(pl.multiple_of(w0, 16), 32)
            rel = win_id - (ln - w0)
            for buf, new in ((kbuf, news[0]), (vbuf, news[1])):
                for kv in range(KV_LOC):
                    val = buf[s, bl, kv, win, :].astype(F32)
                    for t in range(STEPS):
                        row = new[t][bl:bl + 1, kv * HEAD:(kv + 1) * HEAD]
                        val = jnp.where(rel == t, jnp.broadcast_to(row, (32, HEAD)), val)
                    buf[s, bl, kv, win, :] = val.astype(BF16)
        out_copy(i, s, 0).start()
        out_copy(i, s, 1).start()

        zero_q = jnp.zeros((16, HEAD), BF16)
        for bl in range(BBLK):
            ln = len_ref[i * BBLK + bl]
            q_b = q_ref[pl.ds(pl.multiple_of((i * BBLK + bl) * 32, 32), 32), :]
            lhs = jnp.concatenate([jnp.concatenate([q_b[:16], zero_q], axis=1),
                                   jnp.concatenate([zero_q, q_b[16:]], axis=1)], axis=0)
            k_cat = jnp.concatenate([kbuf[s, bl, 0], kbuf[s, bl, 1]], axis=1)
            v_cat = jnp.concatenate([vbuf[s, bl, 0], vbuf[s, bl, 1]], axis=1)
            sc = lax.dot_general(lhs, k_cat, (((1,), (1,)), ((), ())), preferred_element_type=F32) * scale
            sc = jnp.where(gap <= ln, sc, -jnp.inf)
            top = jnp.max(sc, axis=1, keepdims=True)
            ex = jnp.exp(sc - top)
            den = jnp.sum(ex, axis=1, keepdims=True)
            mix = jnp.dot(ex.astype(BF16), v_cat, preferred_element_type=F32)
            o32[bl * 32:bl * 32 + 16, :] = mix[:16, :HEAD] / den[:16]
            o32[bl * 32 + 16:bl * 32 + 32, :] = mix[16:, HEAD:] / den[16:]
        for t in range(STEPS):
            for hd in range(Q_LOC):
                row = (hd // GROUP) * 16 + t * GROUP + hd % GROUP
                slab = o32[pl.ds(row, BBLK, stride=32), :]
                o_ref[t, pl.ds(pl.multiple_of(i * BBLK, BBLK), BBLK), hd * HEAD:(hd + 1) * HEAD] = slab.astype(BF16)
        return 0

    lax.fori_loop(0, N_BLK, block, 0)
    for i in range(N_BLK - 2, N_BLK):
        out_copy(i, i % SLOTS, 0).wait()
        out_copy(i, i % SLOTS, 1).wait()


def run_attn(lengths, q32, k_new, v_new, k_cache, v_cache):
    return pl.pallas_call(
        attn_kernel,
        out_shape=(jax.ShapeDtypeStruct((STEPS, BATCH, Q_LOC * HEAD), BF16),
                   jax.ShapeDtypeStruct(k_cache.shape, BF16),
                   jax.ShapeDtypeStruct(v_cache.shape, BF16)),
        in_specs=[SM, VM, VM, VM, ANY, ANY],
        out_specs=(VM, ANY, ANY),
        scratch_shapes=[
            pltpu.VMEM((SLOTS, BBLK, KV_LOC, SEQ, HEAD), BF16),
            pltpu.VMEM((SLOTS, BBLK, KV_LOC, SEQ, HEAD), BF16),
            pltpu.VMEM((BBLK * 32, HEAD), F32),
            pltpu.SemaphoreType.DMA((2, SLOTS)),
            pltpu.SemaphoreType.DMA((2, SLOTS)),
        ],
        compiler_params=pltpu.CompilerParams(vmem_limit_bytes=48 * 1024 * 1024),
        name='attend',
    )(lengths, q32, k_new, v_new, k_cache, v_cache)


CHUNKS = (64, 64)
CROWS = tuple(STEPS * n for n in CHUNKS)
PIECES = 10
PW = 256
HALF_T = PIECES
RING = 5
RESID = 9
G_TILES = FF_LOC // 128
G_STREAM = G_TILES - RESID
PHASES = (('w', 2 * PIECES), ('g', G_STREAM), ('d', 2 * PIECES), ('g', G_STREAM), ('d', 2 * PIECES))


def mlp_kernel(o_hbm, x_hbm, wo_hbm, w1_hbm, w3_hbm, w2_hbm, ga_ref, gm_ref,
               y_hbm,
               o_v, xh0, xh1, u0, u1, ps0, ps1, pr0, pr1, s0, s1, r10, r11, r20, r21, a0, a1, ring,
               in_sem, ring_sem, res_sem, out_sem,
               p_send, p_recv, c_send, c_recv, a_send, a_recv):
    me = lax.axis_index('tp')
    core = me % 2
    chip = me // 2
    mate = chip * 2 + (1 - core)
    peer = (1 - chip) * 2 + core
    xh, u_v = (xh0, xh1), (u0, u1)
    p_out, p_in, s_v = (ps0, ps1), (pr0, pr1), (s0, s1)
    r_v = ((r10, r11), (r20, r21))
    a_v = (a0, a1)
    firsts = (0, CHUNKS[0])
    row0 = (0, CROWS[0])

    barrier = pltpu.get_barrier_semaphore()
    for dev in (mate, peer):
        pl.semaphore_signal(barrier, inc=1, device_id={'tp': dev}, device_id_type=MESH)

    bases = []
    total = 0
    for _, n in PHASES:
        bases.append(total)
        total += n

    def out_col(i):
        k = i // 2
        own = i % 2
        half = own * core + (1 - own) * (1 - core)
        return half * HALF_T + k

    def g_tile(s):
        return (s // 2) * 3 + s % 2

    def tile_copies(kind, idx, slot, sem):
        if kind == 'w':
            col = pl.multiple_of(out_col(idx) * PW, PW)
            return [pltpu.make_async_copy(wo_hbm.at[:, pl.ds(col, PW)], ring.at[slot, pl.ds(0, Q_LOC * HEAD), :], sem.at[0])]
        if kind == 'd':
            col = pl.multiple_of(out_col(idx) * PW, PW)
            return [pltpu.make_async_copy(w2_hbm.at[:, pl.ds(col, PW)], ring.at[slot, pl.ds(0, FF_LOC), :], sem.at[0])]
        col = pl.multiple_of(idx * 128, 128)
        return [pltpu.make_async_copy(w1_hbm.at[:, pl.ds(col, 128)], ring.at[slot, :, pl.ds(0, 128)], sem.at[0]),
                pltpu.make_async_copy(w3_hbm.at[:, pl.ds(col, 128)], ring.at[slot, :, pl.ds(128, 128)], sem.at[1])]

    def stream(ph, s, start):
        kind = PHASES[ph][0]
        slot = (bases[ph] + s) % RING
        idx = g_tile(s) if kind == 'g' else s
        for cp in tile_copies(kind, idx, slot, ring_sem.at[slot]):
            if start:
                cp.start()
            else:
                cp.wait()
        return slot

    def refill(ph, s):
        n = PHASES[ph][1]

        @pl.when(s + RING < n)
        def _():
            stream(ph, s + RING, True)

        if ph + 1 < len(PHASES):
            @pl.when(s + RING >= n)
            def _():
                stream(ph + 1, s + RING - n, True)

    o_copies, x_copies = [], []
    for ch in range(2):
        for t in range(STEPS):
            o_copies.append(pltpu.make_async_copy(
                o_hbm.at[t, pl.ds(firsts[ch], CHUNKS[ch]), :],
                o_v.at[pl.ds(row0[ch] + t * CHUNKS[ch], CHUNKS[ch]), :], in_sem.at[0, ch, t]))
            x_copies.append(pltpu.make_async_copy(
                x_hbm.at[t, pl.ds(firsts[ch], CHUNKS[ch]), :],
                xh[ch].at[pl.ds(t * CHUNKS[ch], CHUNKS[ch]), :], in_sem.at[1, ch, t]))
    for cp in o_copies:
        cp.start()
    for n in range(RING):
        stream(0, n, True)
    for cp in x_copies:
        cp.start()

    def mate_copy(ex, ch, k):
        return pltpu.make_async_remote_copy(
            src_ref=p_out[ch].at[k], dst_ref=p_in[ch].at[k], send_sem=p_send.at[ex, ch, k], recv_sem=p_recv.at[ex, ch, k],
            device_id={'tp': mate}, device_id_type=MESH)

    def peer_copy(ex, ch, k):
        return pltpu.make_async_remote_copy(
            src_ref=s_v[ch].at[k], dst_ref=r_v[ex][ch].at[k], send_sem=c_send.at[ex, ch, k], recv_sem=c_recv.at[ex, ch, k],
            device_id={'tp': peer}, device_id_type=MESH)

    def gather_copy(ex, ch, k, half):
        j = half * HALF_T + k
        return pltpu.make_async_remote_copy(
            src_ref=a_v[ch].at[j], dst_ref=a_v[ch].at[j], send_sem=a_send.at[ex, ch, k], recv_sem=a_recv.at[ex, ch, k],
            device_id={'tp': mate}, device_id_type=MESH)

    def pair_sum(ex, ch, k):
        mate_copy(ex, ch, k).wait_recv()
        s_v[ch][k] = (s_v[ch][k].astype(F32) + p_in[ch][k].astype(F32)).astype(BF16)

    def full_sum(ex, ch, k):
        peer_copy(ex, ch, k).wait()
        a_v[ch][core * HALF_T + k] = (s_v[ch][k].astype(F32) + r_v[ex][ch][k].astype(F32)).astype(BF16)
        gather_copy(ex, ch, k, core).start()

    def gather_done(ex, ch):
        def step(k, _):
            gather_copy(ex, ch, k, core).wait_send()
            gather_copy(ex, ch, k, 1 - core).wait_recv()
            mate_copy(ex, ch, k).wait_send()
            return 0
        lax.fori_loop(0, PIECES, step, 0)

    def full_sums(ex, ch):
        def step(k, _):
            full_sum(ex, ch, k)
            return 0
        lax.fori_loop(0, PIECES, step, 0)

    def norm_add(ch, gain_ref):
        def step(b, _):
            rows = pl.ds(pl.multiple_of(b * 16, 16), 16)
            acc = jnp.zeros((16, PW), F32)
            for j in range(2 * PIECES):
                val = a_v[ch][j, rows, :].astype(F32)
                acc = acc + val * val
            fac = lax.rsqrt(jnp.sum(acc, axis=1, keepdims=True) / float(D_MODEL) + NORM_EPS)
            for j in range(2 * PIECES):
                cols = slice(j * PW, (j + 1) * PW)
                val = a_v[ch][j, rows, :].astype(F32)
                base = xh[ch][rows, cols].astype(F32)
                xh[ch][rows, cols] = (base + val * fac * gain_ref[:, cols]).astype(BF16)
            return 0
        lax.fori_loop(0, CROWS[ch] // 16, step, 0)

    for cp in o_copies:
        cp.wait()

    def wo_tile(i):
        slot = stream(0, i, False)
        res = jnp.dot(o_v[...], ring[slot, pl.ds(0, Q_LOC * HEAD), :], preferred_element_type=F32).astype(BF16)
        refill(0, i)
        return res

    def wo_step(k, _):
        res = wo_tile(2 * k)
        for ch in range(2):
            p_out[ch][k] = res[row0[ch]:row0[ch] + CROWS[ch]]
            mate_copy(0, ch, k).start()
        res = wo_tile(2 * k + 1)
        for ch in range(2):
            s_v[ch][k] = res[row0[ch]:row0[ch] + CROWS[ch]]

        @pl.when(k >= 1)
        def _():
            pair_sum(0, 0, k - 1)
            peer_copy(0, 0, k - 1).start()
            pair_sum(0, 1, k - 1)
        return 0

    pl.semaphore_wait(barrier, 2)
    lax.fori_loop(0, PIECES, wo_step, 0)
    pair_sum(0, 0, PIECES - 1)
    peer_copy(0, 0, PIECES - 1).start()
    pair_sum(0, 1, PIECES - 1)

    def send_b(k, _):
        peer_copy(0, 1, k).start()
        return 0
    lax.fori_loop(0, PIECES, send_b, 0)

    def res_load(r, _):
        for cp in tile_copies('g', r * 3 + 2, RING + r, res_sem.at[r]):
            cp.start()
        return 0
    lax.fori_loop(0, RESID, res_load, 0)
    for cp in x_copies:
        cp.wait()

    full_sums(0, 0)
    gather_done(0, 0)
    norm_add(0, ga_ref)

    def res_wait(r, _):
        for cp in tile_copies('g', r * 3 + 2, RING + r, res_sem.at[r]):
            cp.wait()
        return 0
    lax.fori_loop(0, RESID, res_wait, 0)

    def gate_up(ph, ch):
        def tile(i, slot):
            acc = jnp.dot(xh[ch][...], ring[slot], preferred_element_type=F32)
            gate = acc[:, :128]
            act = (gate * jax.nn.sigmoid(gate)) * acc[:, 128:]
            u_v[ch][:, pl.ds(pl.multiple_of(i * 128, 128), 128)] = act.astype(BF16)

        def step(i, _):
            q = i // 3
            m = i % 3
            s = 2 * q + m

            @pl.when(m < 2)
            def _():
                stream(ph, s, False)
            slot = jnp.where(m == 2, RING + q, (bases[ph] + s) % RING)
            tile(i, slot)

            @pl.when(m < 2)
            def _():
                refill(ph, s)
            return 0
        lax.fori_loop(0, G_TILES, step, 0)

    def down(ph, ch, also):
        def d_tile(i):
            slot = stream(ph, i, False)
            res = jnp.dot(u_v[ch][...], ring[slot, pl.ds(0, FF_LOC), :], preferred_element_type=F32).astype(BF16)
            refill(ph, i)
            return res

        def step(k, _):
            p_out[ch][k] = d_tile(2 * k)
            mate_copy(1, ch, k).start()
            s_v[ch][k] = d_tile(2 * k + 1)

            @pl.when(k >= 1)
            def _():
                pair_sum(1, ch, k - 1)
                peer_copy(1, ch, k - 1).start()
            if also is not None:
                also(k)
            return 0
        lax.fori_loop(0, PIECES, step, 0)
        pair_sum(1, ch, PIECES - 1)
        peer_copy(1, ch, PIECES - 1).start()

    gate_up(1, 0)
    down(2, 0, lambda k: full_sum(0, 1, k))
    gather_done(0, 1)
    norm_add(1, ga_ref)
    gate_up(3, 1)
    down(4, 1, lambda k: full_sum(1, 0, k))

    def y_copies(ch):
        return [pltpu.make_async_copy(xh[ch].at[pl.ds(t * CHUNKS[ch], CHUNKS[ch]), :],
                                      y_hbm.at[t, pl.ds(firsts[ch], CHUNKS[ch]), :], out_sem.at[ch, t]) for t in range(STEPS)]

    gather_done(1, 0)
    norm_add(0, gm_ref)
    for cp in y_copies(0):
        cp.start()
    full_sums(1, 1)
    gather_done(1, 1)
    norm_add(1, gm_ref)
    for cp in y_copies(1):
        cp.start()
    for ch in range(2):
        for cp in y_copies(ch):
            cp.wait()


def run_mlp(o, x_seq, w_o, w_gate, w_up, w_down, ga, gm):
    piece = lambda ch: pltpu.VMEM((PIECES, CROWS[ch], PW), BF16)
    sem = pltpu.SemaphoreType.DMA
    return pl.pallas_call(
        mlp_kernel,
        out_shape=jax.ShapeDtypeStruct((STEPS, BATCH, D_MODEL), BF16),
        in_specs=[ANY, ANY, ANY, ANY, ANY, ANY, VM, VM],
        out_specs=ANY,
        scratch_shapes=[
            pltpu.VMEM((ROWS, Q_LOC * HEAD), BF16),
            pltpu.VMEM((CROWS[0], D_MODEL), BF16), pltpu.VMEM((CROWS[1], D_MODEL), BF16),
            pltpu.VMEM((CROWS[0], FF_LOC), BF16), pltpu.VMEM((CROWS[1], FF_LOC), BF16),
            piece(0), piece(1), piece(0), piece(1), piece(0), piece(1),
            piece(0), piece(1), piece(0), piece(1),
            pltpu.VMEM((2 * PIECES, CROWS[0], PW), BF16), pltpu.VMEM((2 * PIECES, CROWS[1], PW), BF16),
            pltpu.VMEM((RING + RESID, D_MODEL, PW), BF16),
            sem((2, 2, STEPS)), sem((RING, 2)), sem((RESID, 2)), sem((2, STEPS)),
            sem((2, 2, PIECES)), sem((2, 2, PIECES)), sem((2, 2, PIECES)),
            sem((2, 2, PIECES)), sem((2, 2, PIECES)), sem((2, 2, PIECES)),
        ],
        compiler_params=pltpu.CompilerParams(collective_id=1, has_side_effects=True, vmem_limit_bytes=67043328),
        name='wo_mlp',
    )(o, x_seq, w_o, w_gate, w_up, w_down, ga, gm)


def solution(mesh):
    def local_run(x_seq, cache_len, k_cache, v_cache, w_q, w_k, w_v, w_o, w_gate, w_up, w_down, g_q, g_k, g_attn, g_mlp):
        inv_freq = ROPE_THETA ** (-(jnp.arange(HEAD // 2, dtype=F32) * (2.0 / HEAD)))
        pos = (cache_len[None, :] + jnp.arange(STEPS, dtype=jnp.int32)[:, None]).reshape(ROWS)
        ang = pos.astype(F32)[:, None] * jnp.concatenate([inv_freq, inv_freq])[None, :]
        cos_t = jnp.cos(ang)
        sin_t = jnp.sin(ang) * jnp.where(jnp.arange(HEAD) < HEAD // 2, -1.0, 1.0).astype(F32)[None, :]
        row = lambda g: g.astype(F32)[None, :]
        q32, k_new, v_new = run_qkv(x_seq.reshape(ROWS, D_MODEL), w_q, w_k, w_v, row(g_q), row(g_k), cos_t, sin_t)
        o, k_out, v_out = run_attn(cache_len, q32, k_new, v_new, k_cache, v_cache)
        y = run_mlp(o, x_seq, w_o, w_gate, w_up, w_down, row(g_attn), row(g_mlp))
        return y, k_out, v_out

    data_spec = P(None, 'dp', None)
    cache_spec = P('dp', 'tp', None, None)
    col_spec = P(None, 'tp')
    row_spec = P('tp', None)
    arg_specs = (data_spec, P('dp'), cache_spec, cache_spec, col_spec, col_spec, col_spec, row_spec, col_spec, col_spec, row_spec, P('tp'), P('tp'), P(None), P(None))
    out_specs = (data_spec, cache_spec, cache_spec)
    return jax.shard_map(local_run, mesh=mesh, in_specs=arg_specs, out_specs=out_specs, check_vma=False)
```

time: 464 us -> 201 us (0.43); the launches traced: 457 us -> 201 us
  matrix products: 232 us -> 0 us
  Pallas kernels: 0 us -> 188 us
  waiting for transfers between devices: 126 us -> 0 us
  other arithmetic: 53.8 us -> 4.78 us
  between operations: 15.2 us -> 0.7 us
  local copies, waits for them, and re-layouts: 20.6 us -> 7.66 us
  blocking collectives: 8.9 us -> 0 us
    dot_general x29 -> x0, matrix products: 232 us -> none  [the longest x3 81.3 us: layer_steps(): jnp.dot(act_loc, w_down, preferred_element_type=jnp.float32)]
    pallas_call x0 -> x3, Pallas kernels: none -> 188 us  [the longest x1 124 us: run_mlp(): pl.pallas_call(mlp_kernel, out_shape=jax.ShapeDtypeStruct((STEPS, BATCH,...]
    psum x2 -> x0, waiting for transfers between devices: 126 us -> none  [group_psum(): return lax.psum(part_val, 'tp')]
    select_n x1, other arithmetic: 23 us -> 0.08 us  [local_run(): jnp.where(jnp.arange(HEAD) < HEAD // 2, -1.0, 1.0).astype(F32)[None, :]]
    reduce_sum x9 -> x0, other arithmetic: 13.8 us -> none  [the longest x3 5.12 us: layer_steps(): jnp.sum(attn_sum * attn_sum, axis=-1, keepdims=True)]
    concatenate x16 -> x0, local copies, waits for them, and re-layouts: 10.8 us -> none  [apply_rope(): jnp.concatenate([lead_half * cos_rows - tail_half * sin_rows, tail_half *...]
    psum x1 -> x0, blocking collectives: 8.9 us -> none  [group_psum(): return lax.psum(part_val, 'tp')]
    another operation x10 -> x0, other arithmetic: 6.02 us -> none  [the longest x2 5.45 us: layer_steps(): return (jnp.stack(y_list), k_out, v_out)]
  transfers between devices with their start and end apart: 2 -> 0, of which waited for: 2 -> 0; matrix products, arithmetic and copies ran while one was open for 5% -> 0% of each run, Pallas kernels for 0% -> 0%
where the time goes in v1:
time: 201 us
  Pallas kernels  188 us (94%)
  local copies, waits for them, and re-layouts  7.66 us (4%)
  other arithmetic  4.78 us (2%)
    pallas_call x1, Pallas kernels, run_mlp(): pl.pallas_call(mlp_kernel, out_shape=jax.ShapeDtypeStruct((STEPS, BATCH,...  124 us
    pallas_call x1, Pallas kernels, run_attn(): pl.pallas_call(attn_kernel, out_shape=(jax.ShapeDtypeStruct((STEPS, BATCH...  42.1 us
    pallas_call x1, Pallas kernels, run_qkv(): pl.pallas_call(qkv_kernel, out_shape=(jax.ShapeDtypeStruct((BATCH * 32, H...  21.6 us
    unnamed x7, local copies, waits for them, and re-layouts  6.97 us

profile of v1, /device:TPU:0, one launch (start us, length us, event | category | flops | bytes accessed | tf_op | source)
XLA Modules:
  0.0 200.9 jit_solution(15995375088532395485)
XLA Ops:
  0.6 0.0 copy-start.2
  0.7 0.1 compare_select_fusion
  0.7 0.7 broadcast_in_dim.44
  1.4 0.7 convert_bitcast_fusion
  2.1 0.7 reshape.32.gq_ref
  2.7 1.3 broadcast_in_dim.45
  4.0 1.3 broadcast_in_dim.46
  5.4 0.8 fusion
  6.1 0.0 copy-start
  6.1 1.7 copy-done
  7.9 21.6 %qkv_rope.1 = (bf16[4096,128]{1,0:T(8,128)(2,1)S(1)}, bf16[384,256]{1,0:T(8,128)(2,1)S(1)}, bf16[384,256]{1,0:T(8,128)(2,1)S(1)}) custom-call(bf16[384,5120]{1,0:T(8,128)(2,1)} %bitcast.7, bf16[5120,1280]{1,0:T(8,128)(2,1)} %wq_hbm.1, bf16[5120,256]{1,0:T(8,128)(2,1)S(1)} %copy-done, bf16[5120,256]{1,0:T(8,128)(2,1)} %wv_hbm.1, ...), custom_call_target="tpu_custom_call" | custom-call | tf_op jit(solution)/shard_map/qkv_rope/pallas_call | solution.py:118
  29.5 0.0 copy-done.2
  29.5 42.1 %attend.1 = (bf16[3,128,1280]{2,1,0:T(8,128)(2,1)S(1)}, bf16[128,2,256,128]{3,2,1,0:T(8,128)(2,1)}, bf16[128,2,256,128]{3,2,1,0:T(8,128)(2,1)}) custom-call(s32[128]{0:T(128)S(1)} %copy-done.2, bf16[4096,128]{1,0:T(8,128)(2,1)S(1)} %get-tuple-element.9.q_ref, bf16[384,256]{1,0:T(8,128)(2,1)S(1)} %get-tuple-element.10.kn_ref, ...), custom_call_target="tpu_custom_call" | custom-call | tf_op jit(solution)/shard_map/attend/pallas_call | solution.py:236
  71.7 0.0 copy-start.1
  71.7 0.9 copy-done.1
  72.6 123.9 %wo_mlp.1 = bf16[3,128,5120]{2,1,0:T(8,128)(2,1)} custom-call(bf16[3,128,1280]{2,1,0:T(8,128)(2,1)} %copy-done.1, bf16[3,128,5120]{2,1,0:T(8,128)(2,1)} %x_hbm.1, bf16[1280,5120]{1,0:T(8,128)(2,1)} %wo_hbm.1, bf16[5120,3456]{1,0:T(8,128)(2,1)} %w1_hbm.1, bf16[5120,3456]{1,0:T(8,128)(2,1)} %w3_hbm.1, bf16[3456,5120]{1,0:T(8,128)(2,1)} %w2_hbm.1, ...), custom_call_target="tpu_custom_call" | custom-call | tf_op jit(solution)/shard_map/wo_mlp/pallas_call | solution.py:537
  196.6 4.3 %copy.19 = bf16[3,128,5120]{2,1,0:T(8,128)(2,1)} copy(bf16[3,128,5120]{2,1,0:T(8,128)(2,1)} %wo_mlp.1) | data formatting | bytes 7864320
  (1 shorter events, 0.0 us)
Async XLA Ops:
  0.6 28.9 %copy-start.2 = (s32[128]{0:T(128)S(1)}, s32[128]{0:T(128)}, u32[]{:S(2)}) copy-start(s32[128]{0:T(128)} %len_ref.1) | copy-start | bytes 1540
  6.1 1.7 copy-start
  71.7 0.9 copy-start.1

commit v2 on v1

v2 whole, which is shorter than its diff:
```python
import jax
import jax.numpy as jnp
import numpy as np
from jax import lax
from jax.experimental import pallas as pl
from jax.experimental.pallas import tpu as pltpu
from jax.sharding import PartitionSpec as P

ROPE_THETA = 500000.0
NORM_EPS = 1e-6
MESH = pl.DeviceIdType.MESH
F32 = jnp.float32
BF16 = jnp.bfloat16

STEPS = 3
BATCH = 128
ROWS = STEPS * BATCH
D_MODEL = 5120
HEAD = 128
KV_LOC = 2
GROUP = 5
Q_LOC = KV_LOC * GROUP
SEQ = 256
FF_LOC = 3456

ANY = pl.BlockSpec(memory_space=pl.ANY)
VM = pl.BlockSpec(memory_space=pltpu.VMEM)
SM = pl.BlockSpec(memory_space=pltpu.SMEM)
HB = pl.BlockSpec(memory_space=pltpu.HBM)


N_TILE = 512


def qkv_kernel(x_hbm, wq_hbm, wk_hbm, wv_hbm, gq_hbm, gk_hbm, len_hbm, freq_hbm,
               q_hbm, k_hbm, v_hbm,
               x_v, w_v, raw, cos_v, sin_v, sq_acc, sq_own, sq_recv, q_v, k_v, v_v, gq_v, gk_v, len_v, freq_v,
               x_sem, w_sem, send_sem, recv_sem, t_sem, o_sem):
    me = lax.axis_index('tp')
    barrier = pltpu.get_barrier_semaphore()
    for d in range(1, 4):
        pl.semaphore_signal(barrier, inc=1, device_id={'tp': (me + d) % 4}, device_id_type=MESH)

    half_k = D_MODEL // 2
    halves = [pl.ds(n * half_k, half_k) for n in range(2)]
    x_copies = [pltpu.make_async_copy(x_hbm.at[:, h], x_v.at[:, h], x_sem.at[n]) for n, h in enumerate(halves)]
    w_copies = [
        [pltpu.make_async_copy(wq_hbm.at[h, pl.ds(0, 512)], w_v.at[0, h], w_sem.at[n]) for n, h in enumerate(halves)],
        [pltpu.make_async_copy(wq_hbm.at[:, pl.ds(512, 512)], w_v.at[1], w_sem.at[2])],
        [pltpu.make_async_copy(wq_hbm.at[:, pl.ds(1024, 256)], w_v.at[2, :, pl.ds(0, 256)], w_sem.at[3]),
         pltpu.make_async_copy(wk_hbm, w_v.at[2, :, pl.ds(256, 256)], w_sem.at[4])],
        [pltpu.make_async_copy(wv_hbm, w_v.at[3, :, pl.ds(0, 256)], w_sem.at[5])],
    ]
    t_copies = [pltpu.make_async_copy(src, dst, t_sem.at[n])
                for n, (src, dst) in enumerate(((len_hbm, len_v), (freq_hbm, freq_v), (gq_hbm, gq_v), (gk_hbm, gk_v)))]
    for cp in t_copies:
        cp.start()
    for n in range(2):
        x_copies[n].start()
        w_copies[0][n].start()

    for cp in t_copies:
        cp.wait()
    len_col = jnp.transpose(jnp.broadcast_to(len_v[...].astype(F32), (HEAD, BATCH)))
    sign = jnp.where(lax.broadcasted_iota(jnp.int32, (BATCH, HEAD), 1) < HEAD // 2, -1.0, 1.0)
    for t in range(STEPS):
        rows = pl.ds(t * BATCH, BATCH)
        ang = (len_col + float(t)) * freq_v[...]
        cos_v[rows, :] = jnp.cos(ang)
        sin_v[rows, :] = jnp.sin(ang) * sign

    def piece(col, rows):
        return raw[col // N_TILE, rows, col % N_TILE:col % N_TILE + HEAD]

    def square(cols, rows, acc):
        for col in cols:
            val = piece(col, rows)
            acc = acc + val * val
        return acc

    all_rows = [pl.ds(t * BATCH, BATCH) for t in range(STEPS)]
    zero = jnp.zeros((BATCH, HEAD), F32)

    with jax.named_scope('k1_w0'):
        x_copies[0].wait()
        w_copies[0][0].wait()
    w_copies[1][0].start()
    part = jnp.dot(x_v[:, halves[0]], w_v[0, halves[0], :], preferred_element_type=F32)
    raw[0] = part
    x_copies[1].wait()
    w_copies[0][1].wait()
    for cp in w_copies[2]:
        cp.start()
    part = jnp.dot(x_v[:, halves[1]], w_v[0, halves[1], :], preferred_element_type=F32)
    raw[0] = (raw[0] + part).astype(BF16).astype(F32)
    w_copies[1][0].wait()
    w_copies[3][0].start()
    raw[1] = jnp.dot(x_v[...], w_v[1], preferred_element_type=F32).astype(BF16).astype(F32)
    w_copies[2][0].wait()
    w_copies[2][1].wait()
    for t in range(STEPS):
        sq_acc[all_rows[t], :] = square(range(0, 1024, HEAD), all_rows[t], zero)
    raw[2] = jnp.dot(x_v[...], w_v[2], preferred_element_type=F32).astype(BF16).astype(F32)
    w_copies[3][0].wait()

    first_row = lax.broadcasted_iota(jnp.int32, (8, BATCH), 0) == 0
    for t in range(STEPS):
        rows = all_rows[t]
        sums = [jnp.sum(jnp.transpose(acc), axis=0, keepdims=True)
                for acc in (square(range(1024, 1280, HEAD), rows, sq_acc[rows, :]), square(range(1280, 1536, HEAD), rows, zero))]
        sq_own[:, t * BATCH:(t + 1) * BATCH] = jnp.where(first_row, sums[0], sums[1])

    with jax.named_scope('k1_barrier'):
        pl.semaphore_wait(barrier, 3)
    copies = []
    for d in range(1, 4):
        cp = pltpu.make_async_remote_copy(
            src_ref=sq_own, dst_ref=sq_recv.at[d - 1], send_sem=send_sem.at[d - 1], recv_sem=recv_sem.at[d - 1],
            device_id={'tp': (me + d) % 4}, device_id_type=MESH)
        cp.start()
        copies.append(cp)
    v_v[...] = jnp.dot(x_v[...], w_v[3, :, pl.ds(0, 256)], preferred_element_type=F32).astype(BF16)
    outs = [pltpu.make_async_copy(v_v, v_hbm, o_sem.at[0])]
    outs[0].start()
    with jax.named_scope('k1_recv'):
        for cp in copies:
            cp.wait()

    q_width = float(Q_LOC * HEAD * 4)
    k_width = float(KV_LOC * HEAD * 4)
    for t in range(STEPS):
        cols = slice(t * BATCH, (t + 1) * BATCH)
        rows = all_rows[t]
        tot = sq_own[:, cols] + sq_recv[0, :, cols] + sq_recv[1, :, cols] + sq_recv[2, :, cols]
        q_fac = lax.rsqrt(tot[0:1] / q_width + NORM_EPS)
        k_fac = lax.rsqrt(tot[1:2] / k_width + NORM_EPS)
        q_col = jnp.transpose(jnp.broadcast_to(q_fac, (HEAD, BATCH)))
        k_col = jnp.transpose(jnp.broadcast_to(k_fac, (HEAD, BATCH)))
        cos_t = cos_v[rows, :]
        sin_t = sin_v[rows, :]
        for hd in range(Q_LOC):
            val = piece(hd * HEAD, rows) * q_col * gq_v[hd:hd + 1, :].astype(F32)
            rot = val * cos_t + pltpu.roll(val, HEAD // 2, 1) * sin_t
            q_v[(hd // GROUP) * 15 + t * GROUP + hd % GROUP] = rot.astype(BF16)
        for kv in range(KV_LOC):
            val = piece((Q_LOC + kv) * HEAD, rows) * k_col * gk_v[kv:kv + 1, :].astype(F32)
            rot = val * cos_t + pltpu.roll(val, HEAD // 2, 1) * sin_t
            k_v[rows, kv * HEAD:(kv + 1) * HEAD] = rot.astype(BF16)
        for kv in range(KV_LOC):
            slabs = pl.ds(kv * 15 + t * GROUP, GROUP)
            outs.append(pltpu.make_async_copy(q_v.at[slabs], q_hbm.at[slabs], o_sem.at[len(outs)]))
        outs.append(pltpu.make_async_copy(k_v.at[rows], k_hbm.at[rows], o_sem.at[len(outs)]))
        for cp in outs[-3:]:
            cp.start()
    with jax.named_scope('k1_out'):
        for cp in outs:
            cp.wait()


def run_qkv(x2, w_q, w_k, w_v, g_q, g_k, len_row, freq_row):
    return pl.pallas_call(
        qkv_kernel,
        out_shape=(jax.ShapeDtypeStruct((30, BATCH, HEAD), BF16),
                   jax.ShapeDtypeStruct((ROWS, KV_LOC * HEAD), BF16),
                   jax.ShapeDtypeStruct((ROWS, KV_LOC * HEAD), BF16)),
        in_specs=[HB] * 8,
        out_specs=(HB, HB, HB),
        scratch_shapes=[
            pltpu.VMEM((ROWS, D_MODEL), BF16),
            pltpu.VMEM((4, D_MODEL, N_TILE), BF16),
            pltpu.VMEM((3, ROWS, N_TILE), F32),
            pltpu.VMEM((ROWS, HEAD), F32),
            pltpu.VMEM((ROWS, HEAD), F32),
            pltpu.VMEM((ROWS, HEAD), F32),
            pltpu.VMEM((8, ROWS), F32),
            pltpu.VMEM((3, 8, ROWS), F32),
            pltpu.VMEM((30, BATCH, HEAD), BF16),
            pltpu.VMEM((ROWS, KV_LOC * HEAD), BF16),
            pltpu.VMEM((ROWS, KV_LOC * HEAD), BF16),
            pltpu.VMEM((Q_LOC, HEAD), BF16),
            pltpu.VMEM((KV_LOC, HEAD), BF16),
            pltpu.VMEM((1, BATCH), jnp.int32),
            pltpu.VMEM((1, HEAD), F32),
            pltpu.SemaphoreType.DMA((2,)),
            pltpu.SemaphoreType.DMA((6,)),
            pltpu.SemaphoreType.DMA((3,)),
            pltpu.SemaphoreType.DMA((3,)),
            pltpu.SemaphoreType.DMA((4,)),
            pltpu.SemaphoreType.DMA((10,)),
        ],
        compiler_params=pltpu.CompilerParams(collective_id=0, has_side_effects=True, vmem_limit_bytes=67043328),
        name='qkv_rope',
    )(x2, w_q, w_k, w_v, g_q, g_k, len_row, freq_row)


BBLK = 16
N_BLK = BATCH // BBLK
SLOTS = 4


def attn_kernel(len_ref, q_hbm, kn_hbm, vn_hbm, kc_hbm, vc_hbm,
                o_hbm, ko_hbm, vo_hbm,
                kbuf, vbuf, q32, o32, sc_v, ex_v, den_v, o_buf, q_ref, kn_ref, vn_ref, in_sem, out_sem, o_sem, t_sem):
    def in_copy(i, s, which):
        src = (kc_hbm, vc_hbm)[which]
        dst = (kbuf, vbuf)[which]
        return pltpu.make_async_copy(src.at[pl.ds(i * BBLK, BBLK)], dst.at[s], in_sem.at[which, s])

    def out_copy(i, s, which):
        dst = (ko_hbm, vo_hbm)[which]
        src = (kbuf, vbuf)[which]
        return pltpu.make_async_copy(src.at[s], dst.at[pl.ds(i * BBLK, BBLK)], out_sem.at[which, s])

    def o_copy(i, t):
        return pltpu.make_async_copy(o_buf.at[i % 2, t], o_hbm.at[t, pl.ds(pl.multiple_of(i * BBLK, BBLK), BBLK), :], o_sem.at[i % 2, t])

    t_copies = [pltpu.make_async_copy(src, dst, t_sem.at[n])
                for n, (src, dst) in enumerate(((kn_hbm, kn_ref), (vn_hbm, vn_ref), (q_hbm, q_ref)))]
    for cp in t_copies:
        cp.start()
    for i in range(2):
        in_copy(i, i, 0).start()
        in_copy(i, i, 1).start()
    for pad in (15, 31):
        q32[pl.ds(pad, BBLK, stride=32), :] = jnp.zeros((BBLK, HEAD), F32)

    scale = HEAD ** -0.5
    row_id = lax.broadcasted_iota(jnp.int32, (32, SEQ), 0)
    col_id = lax.broadcasted_iota(jnp.int32, (32, SEQ), 1)
    sub = row_id - jnp.where(row_id >= 16, 16, 0)
    step_of = jnp.where(sub >= 5, 1, 0) + jnp.where(sub >= 10, 1, 0)
    gap = col_id - step_of
    win_id = lax.broadcasted_iota(jnp.int32, (32, HEAD), 0)

    for cp in t_copies:
        cp.wait()

    def block(i, _):
        s = i % SLOTS

        @pl.when(i >= 2)
        def _():
            out_copy(i - 2, (i + 2) % SLOTS, 0).wait()
            out_copy(i - 2, (i + 2) % SLOTS, 1).wait()
            for t in range(STEPS):
                o_copy(i - 2, t).wait()

        @pl.when(i + 2 < N_BLK)
        def _():
            in_copy(i + 2, (i + 2) % SLOTS, 0).start()
            in_copy(i + 2, (i + 2) % SLOTS, 1).start()

        in_copy(i, s, 0).wait()
        in_copy(i, s, 1).wait()

        news = []
        for src in (kn_ref, vn_ref):
            news.append([src[pl.ds(pl.multiple_of(t * BATCH + i * BBLK, BBLK), BBLK), :].astype(F32) for t in range(STEPS)])
        for bl in range(BBLK):
            ln = len_ref[i * BBLK + bl]
            w0 = jnp.minimum((ln // 16) * 16, SEQ - 32)
            win = pl.ds(pl.multiple_of(w0, 16), 32)
            rel = win_id - (ln - w0)
            for buf, new in ((kbuf, news[0]), (vbuf, news[1])):
                for kv in range(KV_LOC):
                    val = buf[s, bl, kv, win, :].astype(F32)
                    for t in range(STEPS):
                        row = new[t][bl:bl + 1, kv * HEAD:(kv + 1) * HEAD]
                        val = jnp.where(rel == t, jnp.broadcast_to(row, (32, HEAD)), val)
                    buf[s, bl, kv, win, :] = val.astype(BF16)
        out_copy(i, s, 0).start()
        out_copy(i, s, 1).start()

        zero_q = jnp.zeros((16, HEAD), BF16)
        for row in range(30):
            q32[pl.ds(row + row // 15, BBLK, stride=32), :] = q_ref[row, pl.ds(pl.multiple_of(i * BBLK, BBLK), BBLK), :].astype(F32)
        for bl in range(BBLK):
            ln = len_ref[i * BBLK + bl]
            q_b = q32[bl * 32:(bl + 1) * 32, :].astype(BF16)
            lhs = jnp.concatenate([jnp.concatenate([q_b[:16], zero_q], axis=1),
                                   jnp.concatenate([zero_q, q_b[16:]], axis=1)], axis=0)
            k_cat = jnp.concatenate([kbuf[s, bl, 0], kbuf[s, bl, 1]], axis=1)
            sc = lax.dot_general(lhs, k_cat, (((1,), (1,)), ((), ())), preferred_element_type=F32) * scale
            sc_v[bl * 32:(bl + 1) * 32, :] = jnp.where(gap <= ln, sc, -jnp.inf)
        for c in range(BBLK // 2):
            rows = slice(c * 64, (c + 1) * 64)
            sc = sc_v[rows, :]
            ex = jnp.exp(sc - jnp.max(sc, axis=1, keepdims=True))
            ex_v[rows, :] = ex.astype(BF16)
            den_v[rows, :] = jnp.broadcast_to(jnp.sum(ex, axis=1, keepdims=True), (64, HEAD))
        for bl in range(BBLK):
            v_cat = jnp.concatenate([vbuf[s, bl, 0], vbuf[s, bl, 1]], axis=1)
            mix = jnp.dot(ex_v[bl * 32:(bl + 1) * 32, :], v_cat, preferred_element_type=F32)
            o32[bl * 32:bl * 32 + 16, :] = mix[:16, :HEAD] / den_v[bl * 32:bl * 32 + 16, :]
            o32[bl * 32 + 16:bl * 32 + 32, :] = mix[16:, HEAD:] / den_v[bl * 32 + 16:bl * 32 + 32, :]
        for t in range(STEPS):
            for hd in range(Q_LOC):
                row = (hd // GROUP) * 16 + t * GROUP + hd % GROUP
                slab = o32[pl.ds(row, BBLK, stride=32), :]
                o_buf[i % 2, t, :, hd * HEAD:(hd + 1) * HEAD] = slab.astype(BF16)
        for t in range(STEPS):
            o_copy(i, t).start()
        return 0

    lax.fori_loop(0, N_BLK, block, 0)
    for i in range(N_BLK - 2, N_BLK):
        out_copy(i, i % SLOTS, 0).wait()
        out_copy(i, i % SLOTS, 1).wait()
        for t in range(STEPS):
            o_copy(i, t).wait()


def run_attn(lengths, q32, k_new, v_new, k_cache, v_cache):
    return pl.pallas_call(
        attn_kernel,
        out_shape=(jax.ShapeDtypeStruct((STEPS, BATCH, Q_LOC * HEAD), BF16),
                   jax.ShapeDtypeStruct(k_cache.shape, BF16),
                   jax.ShapeDtypeStruct(v_cache.shape, BF16)),
        in_specs=[SM, HB, HB, HB, HB, HB],
        out_specs=(HB, HB, HB),
        scratch_shapes=[
            pltpu.VMEM((SLOTS, BBLK, KV_LOC, SEQ, HEAD), BF16),
            pltpu.VMEM((SLOTS, BBLK, KV_LOC, SEQ, HEAD), BF16),
            pltpu.VMEM((BBLK * 32, HEAD), F32),
            pltpu.VMEM((BBLK * 32, HEAD), F32),
            pltpu.VMEM((BBLK * 32, SEQ), F32),
            pltpu.VMEM((BBLK * 32, SEQ), BF16),
            pltpu.VMEM((BBLK * 32, HEAD), F32),
            pltpu.VMEM((2, STEPS, BBLK, Q_LOC * HEAD), BF16),
            pltpu.VMEM((30, BATCH, HEAD), BF16),
            pltpu.VMEM((ROWS, KV_LOC * HEAD), BF16),
            pltpu.VMEM((ROWS, KV_LOC * HEAD), BF16),
            pltpu.SemaphoreType.DMA((2, SLOTS)),
            pltpu.SemaphoreType.DMA((2, SLOTS)),
            pltpu.SemaphoreType.DMA((2, STEPS)),
            pltpu.SemaphoreType.DMA((3,)),
        ],
        compiler_params=pltpu.CompilerParams(vmem_limit_bytes=67043328),
        name='attend',
    )(lengths, q32, k_new, v_new, k_cache, v_cache)


CHUNKS = (64, 64)
CROWS = tuple(STEPS * n for n in CHUNKS)
PIECES = 5
PW = 512
HALF_T = PIECES
RING = 3
RESID = 6
GW = PW // 2
G_TILES = pl.cdiv(FF_LOC, GW)
G_STREAM = G_TILES - RESID
G_EXTRA = G_STREAM - RESID
PHASES = (('g', G_STREAM), ('d', 2 * PIECES), ('g', G_STREAM), ('d', 2 * PIECES))
WO_PER = D_MODEL // (Q_LOC * HEAD)
WO_SLOTS = pl.cdiv(2 * PIECES, WO_PER)
WO_AHEAD = 4


def mlp_kernel(o_hbm, x_hbm, wo_hbm, w1_hbm, w3_hbm, w2_hbm, ga_hbm, gm_hbm,
               y_hbm,
               o_v, xh0, xh1, u0, ps0, ps1, pr0, pr1, r10, r11, r20, r21, a0, a1, ring, ga_ref, gm_ref,
               in_sem, g_sem, wo_sem, ring_sem, res_sem, out_sem,
               p_send, p_recv, c_send, c_recv, a_send, a_recv):
    me = lax.axis_index('tp')
    core = me % 2
    chip = me // 2
    mate = chip * 2 + (1 - core)
    peer = (1 - chip) * 2 + core
    xh = (xh0, xh1)
    u_v = [u0.at[pl.ds(0, n), :] for n in CROWS]
    p_out, p_in = (ps0, ps1), (pr0, pr1)
    r_v = ((r10, r11), (r20, r21))
    a_v = (a0, a1)
    firsts = (0, CHUNKS[0])
    row0 = (0, CROWS[0])

    barrier = pltpu.get_barrier_semaphore()
    for dev in (mate, peer):
        pl.semaphore_signal(barrier, inc=1, device_id={'tp': dev}, device_id_type=MESH)

    bases = []
    total = 0
    for _, n in PHASES:
        bases.append(total)
        total += n

    def out_col(i):
        k = i // 2
        own = i % 2
        half = own * core + (1 - own) * (1 - core)
        return half * HALF_T + k

    def g_col(i):
        return pl.multiple_of(jnp.minimum(i * GW, FF_LOC - GW), 128)

    def g_tile(s):
        return jnp.where(s < G_EXTRA, G_TILES - G_EXTRA + s, 2 * (s - G_EXTRA))

    def tile_copies(kind, idx, slot, sem):
        if kind == 'd':
            col = pl.multiple_of(out_col(idx) * PW, PW)
            return [pltpu.make_async_copy(w2_hbm.at[:, pl.ds(col, PW)], ring.at[slot, pl.ds(0, FF_LOC), :], sem.at[0])]
        col = g_col(idx)
        return [pltpu.make_async_copy(w1_hbm.at[:, pl.ds(col, GW)], ring.at[slot, :, pl.ds(0, GW)], sem.at[0]),
                pltpu.make_async_copy(w3_hbm.at[:, pl.ds(col, GW)], ring.at[slot, :, pl.ds(GW, GW)], sem.at[1])]

    def stream(ph, s, start):
        kind = PHASES[ph][0]
        slot = (bases[ph] + s) % RING
        idx = g_tile(s) if kind == 'g' else s
        for cp in tile_copies(kind, idx, slot, ring_sem.at[slot]):
            if start:
                cp.start()
            else:
                cp.wait()
        return slot

    def refill(ph, s):
        n = PHASES[ph][1]

        @pl.when(s + RING < n)
        def _():
            stream(ph, s + RING, True)

        if ph + 1 < len(PHASES):
            @pl.when(s + RING >= n)
            def _():
                stream(ph + 1, s + RING - n, True)

    o_copies, x_copies = [], []
    for ch in range(2):
        for t in range(STEPS):
            o_copies.append(pltpu.make_async_copy(
                o_hbm.at[t, pl.ds(firsts[ch], CHUNKS[ch]), :],
                o_v.at[pl.ds(row0[ch] + t * CHUNKS[ch], CHUNKS[ch]), :], in_sem.at[0, ch, t]))
            x_copies.append(pltpu.make_async_copy(
                x_hbm.at[t, pl.ds(firsts[ch], CHUNKS[ch]), :],
                xh[ch].at[pl.ds(t * CHUNKS[ch], CHUNKS[ch]), :], in_sem.at[1, ch, t]))
    g_copies = [pltpu.make_async_copy(ga_hbm, ga_ref, g_sem.at[0]), pltpu.make_async_copy(gm_hbm, gm_ref, g_sem.at[1])]
    for cp in o_copies + g_copies:
        cp.start()
    def wo_copy(i):
        col = pl.multiple_of(out_col(i) * PW, PW)
        rows = pl.ds(pl.multiple_of((i % WO_PER) * (Q_LOC * HEAD), Q_LOC * HEAD), Q_LOC * HEAD)
        return pltpu.make_async_copy(wo_hbm.at[:, pl.ds(col, PW)], ring.at[RING + i // WO_PER, rows, :], wo_sem.at[i])

    def res_copies(r):
        return tile_copies('g', 2 * r + 1, RING + r, res_sem.at[r])

    for i in range(WO_AHEAD):
        wo_copy(i).start()

    def mate_copy(ex, ch, k):
        return pltpu.make_async_remote_copy(
            src_ref=p_out[ch].at[k], dst_ref=p_in[ch].at[k], send_sem=p_send.at[ex, ch, k], recv_sem=p_recv.at[ex, ch, k],
            device_id={'tp': mate}, device_id_type=MESH)

    def peer_copy(ex, ch, k):
        return pltpu.make_async_remote_copy(
            src_ref=a_v[ch].at[core * HALF_T + k], dst_ref=r_v[ex][ch].at[k], send_sem=c_send.at[ex, ch, k], recv_sem=c_recv.at[ex, ch, k],
            device_id={'tp': peer}, device_id_type=MESH)

    def gather_copy(ex, ch, k, half):
        j = half * HALF_T + k
        return pltpu.make_async_remote_copy(
            src_ref=a_v[ch].at[j], dst_ref=a_v[ch].at[j], send_sem=a_send.at[ex, ch, k], recv_sem=a_recv.at[ex, ch, k],
            device_id={'tp': mate}, device_id_type=MESH)

    def pair_sum(ex, ch, k):
        mate_copy(ex, ch, k).wait_recv()
        own = core * HALF_T + k
        a_v[ch][own] = (a_v[ch][own].astype(F32) + p_in[ch][k].astype(F32)).astype(BF16)

    def full_sum(ex, ch, k):
        peer_copy(ex, ch, k).wait()
        own = core * HALF_T + k
        a_v[ch][own] = (a_v[ch][own].astype(F32) + r_v[ex][ch][k].astype(F32)).astype(BF16)
        gather_copy(ex, ch, k, core).start()

    def gather_done(ex, ch):
        def step(k, _):
            gather_copy(ex, ch, k, core).wait_send()
            gather_copy(ex, ch, k, 1 - core).wait_recv()
            mate_copy(ex, ch, k).wait_send()
            return 0
        lax.fori_loop(0, PIECES, step, 0)

    def full_sums(ex, ch):
        def step(k, _):
            full_sum(ex, ch, k)
            return 0
        lax.fori_loop(0, PIECES, step, 0)

    def norm_add(ch, gain_ref):
        def step(b, _):
            rows = pl.ds(pl.multiple_of(b * 16, 16), 16)
            acc = jnp.zeros((16, PW), F32)
            for j in range(2 * PIECES):
                val = a_v[ch][j, rows, :].astype(F32)
                acc = acc + val * val
            fac = lax.rsqrt(jnp.sum(acc, axis=1, keepdims=True) / float(D_MODEL) + NORM_EPS)
            for j in range(D_MODEL // HEAD):
                cols = slice(j * HEAD, (j + 1) * HEAD)
                val = a_v[ch][j * HEAD // PW, rows, j * HEAD % PW:j * HEAD % PW + HEAD].astype(F32)
                base = xh[ch][rows, cols].astype(F32)
                xh[ch][rows, cols] = (base + val * fac * gain_ref[j:j + 1, :].astype(F32)).astype(BF16)
            return 0
        lax.fori_loop(0, CROWS[ch] // 16, step, 0)

    for cp in o_copies + g_copies:
        cp.wait()

    def wo_tile(i):
        rows = pl.ds(pl.multiple_of((i % WO_PER) * (Q_LOC * HEAD), Q_LOC * HEAD), Q_LOC * HEAD)
        return jnp.dot(o_v[...], ring[RING + i // WO_PER, rows, :], preferred_element_type=F32).astype(BF16)

    def wo_pair(k):
        for ch in range(2):
            pair_sum(0, ch, k)
        peer_copy(0, 0, k).start()

    def wo_step(k, _):
        wo_copy(2 * k).wait()
        wo_copy(2 * k + 1).wait()

        @pl.when(2 * k + WO_AHEAD < 2 * PIECES)
        def _():
            wo_copy(2 * k + WO_AHEAD).start()
            wo_copy(2 * k + WO_AHEAD + 1).start()
        res = wo_tile(2 * k)
        for ch in range(2):
            p_out[ch][k] = res[row0[ch]:row0[ch] + CROWS[ch]]
            mate_copy(0, ch, k).start()
        res = wo_tile(2 * k + 1)
        for ch in range(2):
            a_v[ch][core * HALF_T + k] = res[row0[ch]:row0[ch] + CROWS[ch]]

        @pl.when(k >= 1)
        def _():
            wo_pair(k - 1)
        return 0

    pl.semaphore_wait(barrier, 2)
    with jax.named_scope('wo'):
        lax.fori_loop(0, PIECES, wo_step, 0)
        wo_pair(PIECES - 1)

    for cp in x_copies:
        cp.start()
    for n in range(RING):
        stream(0, n, True)
    for r in range(RESID):
        for cp in res_copies(r):
            cp.start()
    for cp in x_copies:
        cp.wait()

    def first_sums(k, _):
        full_sum(0, 0, k)
        peer_copy(0, 1, k).start()
        return 0
    with jax.named_scope('sums_a1'):
        lax.fori_loop(0, PIECES, first_sums, 0)
    with jax.named_scope('gather_a1'):
        gather_done(0, 0)
    with jax.named_scope('norm_a1'):
        norm_add(0, ga_ref)

    def gate_up(ph, ch):
        def tile(i, slot):
            acc = jnp.dot(xh[ch][...], ring[slot], preferred_element_type=F32)
            gate = acc[:, :GW]
            act = (gate * jax.nn.sigmoid(gate)) * acc[:, GW:]
            u_v[ch][:, pl.ds(g_col(i), GW)] = act.astype(BF16)

        def single(q, _):
            tile(g_tile(q), stream(ph, q, False))
            refill(ph, q)
            return 0

        def pair(q, _):
            slot = stream(ph, G_EXTRA + q, False)
            if ph == 0:
                for cp in res_copies(q):
                    cp.wait()
            tile(2 * q, slot)
            tile(2 * q + 1, RING + q)
            refill(ph, G_EXTRA + q)
            return 0
        lax.fori_loop(0, G_EXTRA, single, 0)
        lax.fori_loop(0, RESID, pair, 0)

    def down(ph, ch, also):
        def d_tile(i):
            slot = stream(ph, i, False)
            res = jnp.dot(u_v[ch][...], ring[slot, pl.ds(0, FF_LOC), :], preferred_element_type=F32).astype(BF16)
            refill(ph, i)
            return res

        def step(k, _):
            also(k)
            p_out[ch][k] = d_tile(2 * k)
            mate_copy(1, ch, k).start()

            @pl.when(k >= 1)
            def _():
                pair_sum(1, ch, k - 1)
                peer_copy(1, ch, k - 1).start()
            a_v[ch][core * HALF_T + k] = d_tile(2 * k + 1)
            return 0
        lax.fori_loop(0, PIECES, step, 0)

    def down_last(ch):
        pair_sum(1, ch, PIECES - 1)
        peer_copy(1, ch, PIECES - 1).start()

    with jax.named_scope('gate_up_a'):
        gate_up(0, 0)
    with jax.named_scope('down_a'):
        down(1, 0, lambda k: full_sum(0, 1, k))
    with jax.named_scope('gather_b1'):
        gather_done(0, 1)
    with jax.named_scope('norm_b1'):
        norm_add(1, ga_ref)
        down_last(0)
    with jax.named_scope('gate_up_b'):
        gate_up(2, 1)
    with jax.named_scope('down_b'):
        down(3, 1, lambda k: full_sum(1, 0, k))

    def y_copies(ch):
        return [pltpu.make_async_copy(xh[ch].at[pl.ds(t * CHUNKS[ch], CHUNKS[ch]), :],
                                      y_hbm.at[t, pl.ds(firsts[ch], CHUNKS[ch]), :], out_sem.at[ch, t]) for t in range(STEPS)]

    with jax.named_scope('gather_a2'):
        gather_done(1, 0)
    with jax.named_scope('norm_a2'):
        norm_add(0, gm_ref)
        down_last(1)
    for cp in y_copies(0):
        cp.start()
    with jax.named_scope('sums_b2'):
        full_sums(1, 1)
    with jax.named_scope('gather_b2'):
        gather_done(1, 1)
    with jax.named_scope('norm_b2'):
        norm_add(1, gm_ref)
    for cp in y_copies(1):
        cp.start()
    with jax.named_scope('y_out'):
        for ch in range(2):
            for cp in y_copies(ch):
                cp.wait()


def run_mlp(o, x_seq, w_o, w_gate, w_up, w_down, g_a, g_m):
    piece = lambda ch: pltpu.VMEM((PIECES, CROWS[ch], PW), BF16)
    sem = pltpu.SemaphoreType.DMA
    return pl.pallas_call(
        mlp_kernel,
        out_shape=jax.ShapeDtypeStruct((STEPS, BATCH, D_MODEL), BF16),
        in_specs=[HB] * 8,
        out_specs=HB,
        scratch_shapes=[
            pltpu.VMEM((ROWS, Q_LOC * HEAD), BF16),
            pltpu.VMEM((CROWS[0], D_MODEL), BF16), pltpu.VMEM((CROWS[1], D_MODEL), BF16),
            pltpu.VMEM((max(CROWS), FF_LOC), BF16),
            piece(0), piece(1), piece(0), piece(1),
            piece(0), piece(1), piece(0), piece(1),
            pltpu.VMEM((2 * PIECES, CROWS[0], PW), BF16), pltpu.VMEM((2 * PIECES, CROWS[1], PW), BF16),
            pltpu.VMEM((RING + RESID, D_MODEL, PW), BF16),
            pltpu.VMEM((D_MODEL // HEAD, HEAD), BF16), pltpu.VMEM((D_MODEL // HEAD, HEAD), BF16),
            sem((2, 2, STEPS)), sem((2,)), sem((2 * PIECES,)), sem((RING, 2)), sem((RESID, 2)), sem((2, STEPS)),
            sem((2, 2, PIECES)), sem((2, 2, PIECES)), sem((2, 2, PIECES)),
            sem((2, 2, PIECES)), sem((2, 2, PIECES)), sem((2, 2, PIECES)),
        ],
        compiler_params=pltpu.CompilerParams(collective_id=1, has_side_effects=True, vmem_limit_bytes=67043328),
        name='wo_mlp',
    )(o, x_seq, w_o, w_gate, w_up, w_down, g_a, g_m)


def solution(mesh):
    def local_run(x_seq, cache_len, k_cache, v_cache, w_q, w_k, w_v, w_o, w_gate, w_up, w_down, g_q, g_k, g_attn, g_mlp):
        inv_freq = ROPE_THETA ** (-(np.arange(HEAD // 2, dtype=np.float32) * np.float32(2.0 / HEAD)))
        freq_row = jnp.asarray(np.concatenate([inv_freq, inv_freq])[None, :], dtype=F32)
        tiled = lambda g: g.reshape(-1, HEAD)
        q_rot, k_new, v_new = run_qkv(x_seq.reshape(ROWS, D_MODEL), w_q, w_k, w_v, tiled(g_q), tiled(g_k), cache_len[None, :], freq_row)
        o, k_out, v_out = run_attn(cache_len, q_rot, k_new, v_new, k_cache, v_cache)
        y = run_mlp(o, x_seq, w_o, w_gate, w_up, w_down, tiled(g_attn), tiled(g_mlp))
        return y, k_out, v_out

    data_spec = P(None, 'dp', None)
    cache_spec = P('dp', 'tp', None, None)
    col_spec = P(None, 'tp')
    row_spec = P('tp', None)
    arg_specs = (data_spec, P('dp'), cache_spec, cache_spec, col_spec, col_spec, col_spec, row_spec, col_spec, col_spec, row_spec, P('tp'), P('tp'), P(None), P(None))
    out_specs = (data_spec, cache_spec, cache_spec)
    return jax.shard_map(local_run, mesh=mesh, in_specs=arg_specs, out_specs=out_specs, check_vma=False)
```

time: 201 us -> 154 us (0.77)
  Pallas kernels: 188 us -> 149 us
  other arithmetic: 4.78 us -> 0 us
  local copies, waits for them, and re-layouts: 7.66 us -> 4.29 us
    pallas_call x1, Pallas kernels: 42.1 us -> 24.5 us  [run_attn(): pl.pallas_call(attn_kernel, out_shape=(jax.ShapeDtypeStruct((STEPS, BATCH...]
    pallas_call x1, Pallas kernels: 124 us -> 107 us  [run_mlp(): pl.pallas_call(mlp_kernel, out_shape=jax.ShapeDtypeStruct((STEPS, BATCH,...]
    pallas_call x1, Pallas kernels: 21.6 us -> 17.6 us  [run_qkv(): pl.pallas_call(qkv_kernel, out_shape=(jax.ShapeDtypeStruct((30, BATCH, HE...]
    broadcast_in_dim x3 -> x0, other arithmetic: 3.27 us -> none  [local_run(): row = lambda g: g.astype(F32)[None, :]]
    unnamed x7 -> x1, local copies, waits for them, and re-layouts: 6.97 us -> 4.29 us
where the time goes in v2:
time: 154 us
  Pallas kernels  149 us (97%)
  local copies, waits for them, and re-layouts  4.29 us (3%)
    pallas_call x1, Pallas kernels, run_mlp(): pl.pallas_call(mlp_kernel, out_shape=jax.ShapeDtypeStruct((STEPS, BATCH,...  107 us
    pallas_call x1, Pallas kernels, run_attn(): pl.pallas_call(attn_kernel, out_shape=(jax.ShapeDtypeStruct((STEPS, BATCH...  24.5 us
    pallas_call x1, Pallas kernels, run_qkv(): pl.pallas_call(qkv_kernel, out_shape=(jax.ShapeDtypeStruct((30, BATCH, HE...  17.6 us
    unnamed x1, local copies, waits for them, and re-layouts  4.29 us

profile of v2, /device:TPU:0, one launch (start us, length us, event | category | flops | bytes accessed | tf_op | source)
XLA Modules:
  0.0 154.3 jit_solution(3485028984626263827)
XLA Ops:
  0.6 17.6 %qkv_rope.1 = (bf16[30,128,128]{2,1,0:T(8,128)(2,1)}, bf16[384,256]{1,0:T(8,128)(2,1)}, bf16[384,256]{1,0:T(8,128)(2,1)}) custom-call(bf16[384,5120]{1,0:T(8,128)(2,1)} %bitcast.6, bf16[5120,1280]{1,0:T(8,128)(2,1)} %wq_hbm.1, bf16[5120,256]{1,0:T(8,128)(2,1)} %wk_hbm.1, bf16[5120,256]{1,0:T(8,128)(2,1)} %wv_hbm.1, bf16[10,128]{1,0:T(8,128)(2,1)} %bitcast.9, ...), custom_call_target="tpu_custom_call" | custom-call | tf_op jit(solution)/shard_map/qkv_rope/pallas_call | solution.py:161
  18.2 24.5 %attend.1 = (bf16[3,128,1280]{2,1,0:T(8,128)(2,1)}, bf16[128,2,256,128]{3,2,1,0:T(8,128)(2,1)}, bf16[128,2,256,128]{3,2,1,0:T(8,128)(2,1)}) custom-call(s32[128]{0:T(128)} %len_ref.1, bf16[30,128,128]{2,1,0:T(8,128)(2,1)} %get-tuple-element.9.q_hbm, bf16[384,256]{1,0:T(8,128)(2,1)} %get-tuple-element.10.kn_hbm, bf16[384,256]{1,0:T(8,128)(2,1)} %get-tuple-element.11.vn_hbm, ...), custom_call_target="tpu_custom_call" | custom-call | tf_op jit(solution)/shard_map/attend/pallas_call | solution.py:314
  42.7 107.3 %wo_mlp.1 = bf16[3,128,5120]{2,1,0:T(8,128)(2,1)} custom-call(bf16[3,128,1280]{2,1,0:T(8,128)(2,1)} %get-tuple-element.12.o_hbm, bf16[3,128,5120]{2,1,0:T(8,128)(2,1)} %x_hbm.1, bf16[1280,5120]{1,0:T(8,128)(2,1)} %wo_hbm.1, bf16[5120,3456]{1,0:T(8,128)(2,1)} %w1_hbm.1, bf16[5120,3456]{1,0:T(8,128)(2,1)} %w3_hbm.1, bf16[3456,5120]{1,0:T(8,128)(2,1)} %w2_hbm.1, ...), custom_call_target="tpu_custom_call" | custom-call | tf_op jit(solution)/shard_map/wo_mlp/pallas_call | solution.py:660
  150.0 4.3 %copy.20 = bf16[3,128,5120]{2,1,0:T(8,128)(2,1)} copy(bf16[3,128,5120]{2,1,0:T(8,128)(2,1)} %wo_mlp.1) | data formatting | bytes 7864320

commit v3 on v2

--- a/solution.py
+++ b/solution.py
@@ -10,6 +10,8 @@
 NORM_EPS = 1e-6
 MESH = pl.DeviceIdType.MESH
 F32 = jnp.float32
+PAIR = range(2)
+VMEM_ALL = 67043328
 BF16 = jnp.bfloat16
 
 STEPS = 3
@@ -22,6 +24,8 @@
 Q_LOC = KV_LOC * GROUP
 SEQ = 256
 FF_LOC = 3456
+KV_W = KV_LOC * HEAD
+Q_W = Q_LOC * HEAD
 
 ANY = pl.BlockSpec(memory_space=pl.ANY)
 VM = pl.BlockSpec(memory_space=pltpu.VMEM)
@@ -42,11 +46,11 @@
         pl.semaphore_signal(barrier, inc=1, device_id={'tp': (me + d) % 4}, device_id_type=MESH)
 
     half_k = D_MODEL // 2
-    halves = [pl.ds(n * half_k, half_k) for n in range(2)]
+    halves = [pl.ds(n * half_k, half_k) for n in PAIR]
     x_copies = [pltpu.make_async_copy(x_hbm.at[:, h], x_v.at[:, h], x_sem.at[n]) for n, h in enumerate(halves)]
     w_copies = [
-        [pltpu.make_async_copy(wq_hbm.at[h, pl.ds(0, 512)], w_v.at[0, h], w_sem.at[n]) for n, h in enumerate(halves)],
-        [pltpu.make_async_copy(wq_hbm.at[:, pl.ds(512, 512)], w_v.at[1], w_sem.at[2])],
+        [pltpu.make_async_copy(wq_hbm.at[h, pl.ds(0, N_TILE)], w_v.at[0, h], w_sem.at[n]) for n, h in enumerate(halves)],
+        [pltpu.make_async_copy(wq_hbm.at[:, pl.ds(N_TILE, N_TILE)], w_v.at[1], w_sem.at[2])],
         [pltpu.make_async_copy(wq_hbm.at[:, pl.ds(1024, 256)], w_v.at[2, :, pl.ds(0, 256)], w_sem.at[3]),
          pltpu.make_async_copy(wk_hbm, w_v.at[2, :, pl.ds(256, 256)], w_sem.at[4])],
         [pltpu.make_async_copy(wv_hbm, w_v.at[3, :, pl.ds(0, 256)], w_sem.at[5])],
@@ -55,9 +59,8 @@
                 for n, (src, dst) in enumerate(((len_hbm, len_v), (freq_hbm, freq_v), (gq_hbm, gq_v), (gk_hbm, gk_v)))]
     for cp in t_copies:
         cp.start()
-    for n in range(2):
-        x_copies[n].start()
-        w_copies[0][n].start()
+    x_copies[0].start()
+    w_copies[0][0].start()
 
     for cp in t_copies:
         cp.wait()
@@ -69,6 +72,9 @@
         cos_v[rows, :] = jnp.cos(ang)
         sin_v[rows, :] = jnp.sin(ang) * sign
 
+    x_copies[1].start()
+    w_copies[0][1].start()
+
     def piece(col, rows):
         return raw[col // N_TILE, rows, col % N_TILE:col % N_TILE + HEAD]
 
@@ -81,26 +87,33 @@
     all_rows = [pl.ds(t * BATCH, BATCH) for t in range(STEPS)]
     zero = jnp.zeros((BATCH, HEAD), F32)
 
-    with jax.named_scope('k1_w0'):
-        x_copies[0].wait()
-        w_copies[0][0].wait()
+    half_rows = [pl.ds(n * (ROWS // 2), ROWS // 2) for n in PAIR]
+
+    def tile_dot(i, ks=slice(None)):
+        return [jnp.dot(x_v[rows, ks], w_v[i, ks, :], preferred_element_type=F32) for rows in half_rows]
+
+    def keep(i, parts):
+        for rows, part in zip(half_rows, parts):
+            raw[i, rows, :] = part.astype(BF16).astype(F32)
+
+    x_copies[0].wait()
+    w_copies[0][0].wait()
     w_copies[1][0].start()
-    part = jnp.dot(x_v[:, halves[0]], w_v[0, halves[0], :], preferred_element_type=F32)
-    raw[0] = part
+    for rows, part in zip(half_rows, tile_dot(0, halves[0])):
+        raw[0, rows, :] = part
     x_copies[1].wait()
     w_copies[0][1].wait()
     for cp in w_copies[2]:
         cp.start()
-    part = jnp.dot(x_v[:, halves[1]], w_v[0, halves[1], :], preferred_element_type=F32)
-    raw[0] = (raw[0] + part).astype(BF16).astype(F32)
+    keep(0, [raw[0, rows, :] + part for rows, part in zip(half_rows, tile_dot(0, halves[1]))])
     w_copies[1][0].wait()
     w_copies[3][0].start()
-    raw[1] = jnp.dot(x_v[...], w_v[1], preferred_element_type=F32).astype(BF16).astype(F32)
-    w_copies[2][0].wait()
-    w_copies[2][1].wait()
+    keep(1, tile_dot(1))
+    for cp in w_copies[2]:
+        cp.wait()
     for t in range(STEPS):
         sq_acc[all_rows[t], :] = square(range(0, 1024, HEAD), all_rows[t], zero)
-    raw[2] = jnp.dot(x_v[...], w_v[2], preferred_element_type=F32).astype(BF16).astype(F32)
+    keep(2, tile_dot(2))
     w_copies[3][0].wait()
 
     first_row = lax.broadcasted_iota(jnp.int32, (8, BATCH), 0) == 0
@@ -119,7 +132,8 @@
             device_id={'tp': (me + d) % 4}, device_id_type=MESH)
         cp.start()
         copies.append(cp)
-    v_v[...] = jnp.dot(x_v[...], w_v[3, :, pl.ds(0, 256)], preferred_element_type=F32).astype(BF16)
+    for rows in half_rows:
+        v_v[rows, :] = jnp.dot(x_v[rows, :], w_v[3, :, pl.ds(0, 256)], preferred_element_type=F32).astype(BF16)
     outs = [pltpu.make_async_copy(v_v, v_hbm, o_sem.at[0])]
     outs[0].start()
     with jax.named_scope('k1_recv'):
@@ -161,34 +175,27 @@
     return pl.pallas_call(
         qkv_kernel,
         out_shape=(jax.ShapeDtypeStruct((30, BATCH, HEAD), BF16),
-                   jax.ShapeDtypeStruct((ROWS, KV_LOC * HEAD), BF16),
-                   jax.ShapeDtypeStruct((ROWS, KV_LOC * HEAD), BF16)),
+                   jax.ShapeDtypeStruct((ROWS, KV_W), BF16),
+                   jax.ShapeDtypeStruct((ROWS, KV_W), BF16)),
         in_specs=[HB] * 8,
         out_specs=(HB, HB, HB),
         scratch_shapes=[
             pltpu.VMEM((ROWS, D_MODEL), BF16),
             pltpu.VMEM((4, D_MODEL, N_TILE), BF16),
             pltpu.VMEM((3, ROWS, N_TILE), F32),
-            pltpu.VMEM((ROWS, HEAD), F32),
-            pltpu.VMEM((ROWS, HEAD), F32),
-            pltpu.VMEM((ROWS, HEAD), F32),
+            *[pltpu.VMEM((ROWS, HEAD), F32)] * 3,
             pltpu.VMEM((8, ROWS), F32),
             pltpu.VMEM((3, 8, ROWS), F32),
             pltpu.VMEM((30, BATCH, HEAD), BF16),
-            pltpu.VMEM((ROWS, KV_LOC * HEAD), BF16),
-            pltpu.VMEM((ROWS, KV_LOC * HEAD), BF16),
+            pltpu.VMEM((ROWS, KV_W), BF16),
+            pltpu.VMEM((ROWS, KV_W), BF16),
             pltpu.VMEM((Q_LOC, HEAD), BF16),
             pltpu.VMEM((KV_LOC, HEAD), BF16),
             pltpu.VMEM((1, BATCH), jnp.int32),
             pltpu.VMEM((1, HEAD), F32),
-            pltpu.SemaphoreType.DMA((2,)),
-            pltpu.SemaphoreType.DMA((6,)),
-            pltpu.SemaphoreType.DMA((3,)),
-            pltpu.SemaphoreType.DMA((3,)),
-            pltpu.SemaphoreType.DMA((4,)),
-            pltpu.SemaphoreType.DMA((10,)),
+            *[pltpu.SemaphoreType.DMA((n,)) for n in (2, 6, 3, 3, 4, 10)],
         ],
-        compiler_params=pltpu.CompilerParams(collective_id=0, has_side_effects=True, vmem_limit_bytes=67043328),
+        compiler_params=pltpu.CompilerParams(collective_id=0, has_side_effects=True, vmem_limit_bytes=VMEM_ALL),
         name='qkv_rope',
     )(x2, w_q, w_k, w_v, g_q, g_k, len_row, freq_row)
 
@@ -218,9 +225,9 @@
                 for n, (src, dst) in enumerate(((kn_hbm, kn_ref), (vn_hbm, vn_ref), (q_hbm, q_ref)))]
     for cp in t_copies:
         cp.start()
-    for i in range(2):
-        in_copy(i, i, 0).start()
-        in_copy(i, i, 1).start()
+    for i in PAIR:
+        for which in PAIR:
+            in_copy(i, i, which).start()
     for pad in (15, 31):
         q32[pl.ds(pad, BBLK, stride=32), :] = jnp.zeros((BBLK, HEAD), F32)
 
@@ -240,18 +247,18 @@
 
         @pl.when(i >= 2)
         def _():
-            out_copy(i - 2, (i + 2) % SLOTS, 0).wait()
-            out_copy(i - 2, (i + 2) % SLOTS, 1).wait()
+            for which in PAIR:
+                out_copy(i - 2, (i + 2) % SLOTS, which).wait()
             for t in range(STEPS):
                 o_copy(i - 2, t).wait()
 
         @pl.when(i + 2 < N_BLK)
         def _():
-            in_copy(i + 2, (i + 2) % SLOTS, 0).start()
-            in_copy(i + 2, (i + 2) % SLOTS, 1).start()
-
-        in_copy(i, s, 0).wait()
-        in_copy(i, s, 1).wait()
+            for which in PAIR:
+                in_copy(i + 2, (i + 2) % SLOTS, which).start()
+
+        for which in PAIR:
+            in_copy(i, s, which).wait()
 
         news = []
         for src in (kn_ref, vn_ref):
@@ -268,8 +275,8 @@
                         row = new[t][bl:bl + 1, kv * HEAD:(kv + 1) * HEAD]
                         val = jnp.where(rel == t, jnp.broadcast_to(row, (32, HEAD)), val)
                     buf[s, bl, kv, win, :] = val.astype(BF16)
-        out_copy(i, s, 0).start()
-        out_copy(i, s, 1).start()
+        for which in PAIR:
+            out_copy(i, s, which).start()
 
         zero_q = jnp.zeros((16, HEAD), BF16)
         for row in range(30):
@@ -304,8 +311,8 @@
 
     lax.fori_loop(0, N_BLK, block, 0)
     for i in range(N_BLK - 2, N_BLK):
-        out_copy(i, i % SLOTS, 0).wait()
-        out_copy(i, i % SLOTS, 1).wait()
+        for which in PAIR:
+            out_copy(i, i % SLOTS, which).wait()
         for t in range(STEPS):
             o_copy(i, t).wait()
 
@@ -313,7 +320,7 @@
 def run_attn(lengths, q32, k_new, v_new, k_cache, v_cache):
     return pl.pallas_call(
         attn_kernel,
-        out_shape=(jax.ShapeDtypeStruct((STEPS, BATCH, Q_LOC * HEAD), BF16),
+        out_shape=(jax.ShapeDtypeStruct((STEPS, BATCH, Q_W), BF16),
                    jax.ShapeDtypeStruct(k_cache.shape, BF16),
                    jax.ShapeDtypeStruct(v_cache.shape, BF16)),
         in_specs=[SM, HB, HB, HB, HB, HB],
@@ -326,16 +333,16 @@
             pltpu.VMEM((BBLK * 32, SEQ), F32),
             pltpu.VMEM((BBLK * 32, SEQ), BF16),
             pltpu.VMEM((BBLK * 32, HEAD), F32),
-            pltpu.VMEM((2, STEPS, BBLK, Q_LOC * HEAD), BF16),
+            pltpu.VMEM((2, STEPS, BBLK, Q_W), BF16),
             pltpu.VMEM((30, BATCH, HEAD), BF16),
-            pltpu.VMEM((ROWS, KV_LOC * HEAD), BF16),
-            pltpu.VMEM((ROWS, KV_LOC * HEAD), BF16),
+            pltpu.VMEM((ROWS, KV_W), BF16),
+            pltpu.VMEM((ROWS, KV_W), BF16),
             pltpu.SemaphoreType.DMA((2, SLOTS)),
             pltpu.SemaphoreType.DMA((2, SLOTS)),
             pltpu.SemaphoreType.DMA((2, STEPS)),
             pltpu.SemaphoreType.DMA((3,)),
         ],
-        compiler_params=pltpu.CompilerParams(vmem_limit_bytes=67043328),
+        compiler_params=pltpu.CompilerParams(vmem_limit_bytes=VMEM_ALL),
         name='attend',
     )(lengths, q32, k_new, v_new, k_cache, v_cache)
 
@@ -344,6 +351,7 @@
 CROWS = tuple(STEPS * n for n in CHUNKS)
 PIECES = 5
 PW = 512
+D_TILES = PIECES + PIECES
 HALF_T = PIECES
 RING = 3
 RESID = 6
@@ -351,17 +359,20 @@
 G_TILES = pl.cdiv(FF_LOC, GW)
 G_STREAM = G_TILES - RESID
 G_EXTRA = G_STREAM - RESID
-PHASES = (('g', G_STREAM), ('d', 2 * PIECES), ('g', G_STREAM), ('d', 2 * PIECES))
-WO_PER = D_MODEL // (Q_LOC * HEAD)
-WO_SLOTS = pl.cdiv(2 * PIECES, WO_PER)
-WO_AHEAD = 4
+PHASES = (('g', G_STREAM), ('d', D_TILES), ('g', G_STREAM), ('d', D_TILES))
+WO_PER = D_MODEL // Q_W
+WO_SLOTS = pl.cdiv(D_TILES, WO_PER)
+WO_AHEAD = 2
+B_LAG = 2
+WHOLE = 2
+TAIL_ROWS = ((0, 2 * CHUNKS[1]), (2 * CHUNKS[1], CHUNKS[1]))
 
 
 def mlp_kernel(o_hbm, x_hbm, wo_hbm, w1_hbm, w3_hbm, w2_hbm, ga_hbm, gm_hbm,
                y_hbm,
                o_v, xh0, xh1, u0, ps0, ps1, pr0, pr1, r10, r11, r20, r21, a0, a1, ring, ga_ref, gm_ref,
                in_sem, g_sem, wo_sem, ring_sem, res_sem, out_sem,
-               p_send, p_recv, c_send, c_recv, a_send, a_recv):
+               p_send, p_recv, c_send, c_recv, a_send, a_recv, t_send, t_recv):
     me = lax.axis_index('tp')
     core = me % 2
     chip = me // 2
@@ -429,7 +440,7 @@
                 stream(ph + 1, s + RING - n, True)
 
     o_copies, x_copies = [], []
-    for ch in range(2):
+    for ch in PAIR:
         for t in range(STEPS):
             o_copies.append(pltpu.make_async_copy(
                 o_hbm.at[t, pl.ds(firsts[ch], CHUNKS[ch]), :],
@@ -442,7 +453,7 @@
         cp.start()
     def wo_copy(i):
         col = pl.multiple_of(out_col(i) * PW, PW)
-        rows = pl.ds(pl.multiple_of((i % WO_PER) * (Q_LOC * HEAD), Q_LOC * HEAD), Q_LOC * HEAD)
+        rows = pl.ds(pl.multiple_of((i % WO_PER) * Q_W, Q_W), Q_W)
         return pltpu.make_async_copy(wo_hbm.at[:, pl.ds(col, PW)], ring.at[RING + i // WO_PER, rows, :], wo_sem.at[i])
 
     def res_copies(r):
@@ -467,6 +478,21 @@
             src_ref=a_v[ch].at[j], dst_ref=a_v[ch].at[j], send_sem=a_send.at[ex, ch, k], recv_sem=a_recv.at[ex, ch, k],
             device_id={'tp': mate}, device_id_type=MESH)
 
+    def tail_peer(g, k):
+        rows = pl.ds(*TAIL_ROWS[g])
+        return pltpu.make_async_remote_copy(
+            src_ref=a_v[1].at[core * HALF_T + k, rows], dst_ref=r_v[1][1].at[k, rows],
+            send_sem=t_send.at[0, g, k - WHOLE], recv_sem=t_recv.at[0, g, k - WHOLE],
+            device_id={'tp': peer}, device_id_type=MESH)
+
+    def tail_gather(g, k, half):
+        rows = pl.ds(*TAIL_ROWS[g])
+        j = half * HALF_T + k
+        return pltpu.make_async_remote_copy(
+            src_ref=a_v[1].at[j, rows], dst_ref=a_v[1].at[j, rows],
+            send_sem=t_send.at[1, g, k - WHOLE], recv_sem=t_recv.at[1, g, k - WHOLE],
+            device_id={'tp': mate}, device_id_type=MESH)
+
     def pair_sum(ex, ch, k):
         mate_copy(ex, ch, k).wait_recv()
         own = core * HALF_T + k
@@ -492,11 +518,11 @@
             return 0
         lax.fori_loop(0, PIECES, step, 0)
 
-    def norm_add(ch, gain_ref):
+    def norm_add(ch, gain_ref, then=None, steps=range(STEPS)):
         def step(b, _):
             rows = pl.ds(pl.multiple_of(b * 16, 16), 16)
             acc = jnp.zeros((16, PW), F32)
-            for j in range(2 * PIECES):
+            for j in range(D_TILES):
                 val = a_v[ch][j, rows, :].astype(F32)
                 acc = acc + val * val
             fac = lax.rsqrt(jnp.sum(acc, axis=1, keepdims=True) / float(D_MODEL) + NORM_EPS)
@@ -506,64 +532,69 @@
                 base = xh[ch][rows, cols].astype(F32)
                 xh[ch][rows, cols] = (base + val * fac * gain_ref[j:j + 1, :].astype(F32)).astype(BF16)
             return 0
-        lax.fori_loop(0, CROWS[ch] // 16, step, 0)
+        for t in steps:
+            lax.fori_loop(t * CHUNKS[ch] // 16, (t + 1) * CHUNKS[ch] // 16, step, 0)
+            if then is not None:
+                then(t)
 
     for cp in o_copies + g_copies:
         cp.wait()
 
-    def wo_tile(i):
-        rows = pl.ds(pl.multiple_of((i % WO_PER) * (Q_LOC * HEAD), Q_LOC * HEAD), Q_LOC * HEAD)
-        return jnp.dot(o_v[...], ring[RING + i // WO_PER, rows, :], preferred_element_type=F32).astype(BF16)
-
-    def wo_pair(k):
-        for ch in range(2):
+    def wo_tile(i, ch):
+        rows = pl.ds(pl.multiple_of((i % WO_PER) * Q_W, Q_W), Q_W)
+        return jnp.dot(o_v[pl.ds(row0[ch], CROWS[ch]), :], ring[RING + i // WO_PER, rows, :],
+                       preferred_element_type=F32).astype(BF16)
+
+    def wo_sweep(ch):
+        def step(k, _):
+            if ch == 0:
+                wo_copy(2 * k).wait()
+                wo_copy(2 * k + 1).wait()
+
+                @pl.when(2 * k + WO_AHEAD < D_TILES)
+                def _():
+                    wo_copy(2 * k + WO_AHEAD).start()
+                    wo_copy(2 * k + WO_AHEAD + 1).start()
+            p_out[ch][k] = wo_tile(2 * k, ch)
+            mate_copy(0, ch, k).start()
+            a_v[ch][core * HALF_T + k] = wo_tile(2 * k + 1, ch)
+
             pair_sum(0, ch, k)
-        peer_copy(0, 0, k).start()
-
-    def wo_step(k, _):
-        wo_copy(2 * k).wait()
-        wo_copy(2 * k + 1).wait()
-
-        @pl.when(2 * k + WO_AHEAD < 2 * PIECES)
-        def _():
-            wo_copy(2 * k + WO_AHEAD).start()
-            wo_copy(2 * k + WO_AHEAD + 1).start()
-        res = wo_tile(2 * k)
-        for ch in range(2):
-            p_out[ch][k] = res[row0[ch]:row0[ch] + CROWS[ch]]
-            mate_copy(0, ch, k).start()
-        res = wo_tile(2 * k + 1)
-        for ch in range(2):
-            a_v[ch][core * HALF_T + k] = res[row0[ch]:row0[ch] + CROWS[ch]]
-
-        @pl.when(k >= 1)
-        def _():
-            wo_pair(k - 1)
-        return 0
+            if ch == 0:
+                peer_copy(0, ch, k).start()
+            return 0
+        lax.fori_loop(0, PIECES, step, 0)
 
     pl.semaphore_wait(barrier, 2)
     with jax.named_scope('wo'):
-        lax.fori_loop(0, PIECES, wo_step, 0)
-        wo_pair(PIECES - 1)
-
-    for cp in x_copies:
-        cp.start()
-    for n in range(RING):
-        stream(0, n, True)
-    for r in range(RESID):
+        wo_sweep(0)
+        for cp in x_copies:
+            cp.start()
+        for n in range(RING):
+            stream(0, n, True)
+        for r in range(WO_SLOTS, RESID):
+            for cp in res_copies(r):
+                cp.start()
+        wo_sweep(1)
+
+    for r in range(WO_SLOTS):
         for cp in res_copies(r):
             cp.start()
+    with jax.named_scope('sums_a1'):
+        def first_sums(k, _):
+            full_sum(0, 0, k)
+
+            @pl.when(k >= B_LAG)
+            def _():
+                peer_copy(0, 1, k - B_LAG).start()
+            return 0
+        lax.fori_loop(0, PIECES, first_sums, 0)
+        for k in range(PIECES - B_LAG, PIECES):
+            peer_copy(0, 1, k).start()
+    with jax.named_scope('gather_a1'):
+        gather_done(0, 0)
     for cp in x_copies:
         cp.wait()
-
-    def first_sums(k, _):
-        full_sum(0, 0, k)
-        peer_copy(0, 1, k).start()
-        return 0
-    with jax.named_scope('sums_a1'):
-        lax.fori_loop(0, PIECES, first_sums, 0)
-    with jax.named_scope('gather_a1'):
-        gather_done(0, 0)
     with jax.named_scope('norm_a1'):
         norm_add(0, ga_ref)
 
@@ -591,7 +622,11 @@
         lax.fori_loop(0, G_EXTRA, single, 0)
         lax.fori_loop(0, RESID, pair, 0)
 
-    def down(ph, ch, also):
+    def down(ph, ch, also, lag):
+        def swap(k):
+            pair_sum(1, ch, k)
+            peer_copy(1, ch, k).start()
+
         def d_tile(i):
             slot = stream(ph, i, False)
             res = jnp.dot(u_v[ch][...], ring[slot, pl.ds(0, FF_LOC), :], preferred_element_type=F32).astype(BF16)
@@ -603,31 +638,38 @@
             p_out[ch][k] = d_tile(2 * k)
             mate_copy(1, ch, k).start()
 
-            @pl.when(k >= 1)
-            def _():
-                pair_sum(1, ch, k - 1)
-                peer_copy(1, ch, k - 1).start()
+            if lag:
+                @pl.when(k >= 1)
+                def _():
+                    swap(k - 1)
             a_v[ch][core * HALF_T + k] = d_tile(2 * k + 1)
+            if not lag:
+                pair_sum(1, ch, k)
+
+                @pl.when(k < WHOLE)
+                def _():
+                    peer_copy(1, ch, k).start()
             return 0
         lax.fori_loop(0, PIECES, step, 0)
 
-    def down_last(ch):
-        pair_sum(1, ch, PIECES - 1)
-        peer_copy(1, ch, PIECES - 1).start()
 
     with jax.named_scope('gate_up_a'):
         gate_up(0, 0)
     with jax.named_scope('down_a'):
-        down(1, 0, lambda k: full_sum(0, 1, k))
+        down(1, 0, lambda k: full_sum(0, 1, k), True)
     with jax.named_scope('gather_b1'):
         gather_done(0, 1)
     with jax.named_scope('norm_b1'):
         norm_add(1, ga_ref)
-        down_last(0)
+        pair_sum(1, 0, PIECES - 1)
+        peer_copy(1, 0, PIECES - 1).start()
     with jax.named_scope('gate_up_b'):
         gate_up(2, 1)
     with jax.named_scope('down_b'):
-        down(3, 1, lambda k: full_sum(1, 0, k))
+        down(3, 1, lambda k: full_sum(1, 0, k), False)
+        for g in PAIR:
+            for k in range(WHOLE, PIECES):
+                tail_peer(g, k).start()
 
     def y_copies(ch):
         return [pltpu.make_async_copy(xh[ch].at[pl.ds(t * CHUNKS[ch], CHUNKS[ch]), :],
@@ -636,26 +678,44 @@
     with jax.named_scope('gather_a2'):
         gather_done(1, 0)
     with jax.named_scope('norm_a2'):
-        norm_add(0, gm_ref)
-        down_last(1)
-    for cp in y_copies(0):
-        cp.start()
+        norm_add(0, gm_ref, lambda t: y_copies(0)[t].start())
     with jax.named_scope('sums_b2'):
-        full_sums(1, 1)
-    with jax.named_scope('gather_b2'):
-        gather_done(1, 1)
-    with jax.named_scope('norm_b2'):
-        norm_add(1, gm_ref)
-    for cp in y_copies(1):
-        cp.start()
+        def whole_sums(k, _):
+            full_sum(1, 1, k)
+            return 0
+        lax.fori_loop(0, WHOLE, whole_sums, 0)
+    for g in PAIR:
+        rows = pl.ds(*TAIL_ROWS[g])
+        with jax.named_scope(f'sums_b2#g={g}'):
+            for k in range(WHOLE, PIECES):
+                own = core * HALF_T + k
+                tail_peer(g, k).wait()
+                a_v[1][own, rows, :] = (a_v[1][own, rows, :].astype(F32) + r_v[1][1][k, rows, :].astype(F32)).astype(BF16)
+                tail_gather(g, k, core).start()
+        with jax.named_scope(f'gather_b2#g={g}'):
+            if g == 0:
+                def whole_done(k, _):
+                    gather_copy(1, 1, k, core).wait_send()
+                    gather_copy(1, 1, k, 1 - core).wait_recv()
+                    return 0
+                lax.fori_loop(0, WHOLE, whole_done, 0)
+
+                def sends_done(k, _):
+                    mate_copy(1, 1, k).wait_send()
+                    return 0
+                lax.fori_loop(0, PIECES, sends_done, 0)
+            for k in range(WHOLE, PIECES):
+                tail_gather(g, k, core).wait_send()
+                tail_gather(g, k, 1 - core).wait_recv()
+        with jax.named_scope(f'norm_b2#g={g}'):
+            norm_add(1, gm_ref, lambda t: y_copies(1)[t].start(), ((0, 1), (2,))[g])
     with jax.named_scope('y_out'):
-        for ch in range(2):
+        for ch in PAIR:
             for cp in y_copies(ch):
                 cp.wait()
 
 
 def run_mlp(o, x_seq, w_o, w_gate, w_up, w_down, g_a, g_m):
-    piece = lambda ch: pltpu.VMEM((PIECES, CROWS[ch], PW), BF16)
     sem = pltpu.SemaphoreType.DMA
     return pl.pallas_call(
         mlp_kernel,
@@ -663,19 +723,18 @@
         in_specs=[HB] * 8,
         out_specs=HB,
         scratch_shapes=[
-            pltpu.VMEM((ROWS, Q_LOC * HEAD), BF16),
-            pltpu.VMEM((CROWS[0], D_MODEL), BF16), pltpu.VMEM((CROWS[1], D_MODEL), BF16),
+            pltpu.VMEM((ROWS, Q_W), BF16),
+            *[pltpu.VMEM((n, D_MODEL), BF16) for n in CROWS],
             pltpu.VMEM((max(CROWS), FF_LOC), BF16),
-            piece(0), piece(1), piece(0), piece(1),
-            piece(0), piece(1), piece(0), piece(1),
-            pltpu.VMEM((2 * PIECES, CROWS[0], PW), BF16), pltpu.VMEM((2 * PIECES, CROWS[1], PW), BF16),
+            *[pltpu.VMEM((PIECES, n, PW), BF16) for n in CROWS * 4],
+            *[pltpu.VMEM((D_TILES, n, PW), BF16) for n in CROWS],
             pltpu.VMEM((RING + RESID, D_MODEL, PW), BF16),
-            pltpu.VMEM((D_MODEL // HEAD, HEAD), BF16), pltpu.VMEM((D_MODEL // HEAD, HEAD), BF16),
-            sem((2, 2, STEPS)), sem((2,)), sem((2 * PIECES,)), sem((RING, 2)), sem((RESID, 2)), sem((2, STEPS)),
-            sem((2, 2, PIECES)), sem((2, 2, PIECES)), sem((2, 2, PIECES)),
-            sem((2, 2, PIECES)), sem((2, 2, PIECES)), sem((2, 2, PIECES)),
+            *[pltpu.VMEM((D_MODEL // HEAD, HEAD), BF16)] * 2,
+            sem((2, 2, STEPS)), sem((2,)), sem((D_TILES,)), sem((RING, 2)), sem((RESID, 2)), sem((2, STEPS)),
+            *[sem((2, 2, PIECES))] * 6,
+            *[sem((2, 2, PIECES - WHOLE))] * 2,
         ],
-        compiler_params=pltpu.CompilerParams(collective_id=1, has_side_effects=True, vmem_limit_bytes=67043328),
+        compiler_params=pltpu.CompilerParams(collective_id=1, has_side_effects=True, vmem_limit_bytes=VMEM_ALL),
         name='wo_mlp',
     )(o, x_seq, w_o, w_gate, w_up, w_down, g_a, g_m)
 

time: 154 us -> 150 us (0.974)
  Pallas kernels: 149 us -> 145 us
    pallas_call x1, Pallas kernels: 107 us -> 104 us  [run_mlp(): pl.pallas_call(mlp_kernel, out_shape=jax.ShapeDtypeStruct((STEPS, BATCH,...]
where the time goes in v3:
time: 150 us
  Pallas kernels  145 us (97%)
  local copies, waits for them, and re-layouts  4.29 us (3%)
    pallas_call x1, Pallas kernels, run_mlp(): pl.pallas_call(mlp_kernel, out_shape=jax.ShapeDtypeStruct((STEPS, BATCH,...  104 us
    pallas_call x1, Pallas kernels, run_attn(): pl.pallas_call(attn_kernel, out_shape=(jax.ShapeDtypeStruct((STEPS, BATCH...  24.5 us
    pallas_call x1, Pallas kernels, run_qkv(): pl.pallas_call(qkv_kernel, out_shape=(jax.ShapeDtypeStruct((30, BATCH, HE...  16.9 us
    unnamed x1, local copies, waits for them, and re-layouts  4.29 us

profile of v3, /device:TPU:0, one launch (start us, length us, event | category | flops | bytes accessed | tf_op | source)
XLA Modules:
  0.0 149.9 jit_solution(6912064631917148225)
XLA Ops:
  0.6 16.9 %qkv_rope.1 = (bf16[30,128,128]{2,1,0:T(8,128)(2,1)}, bf16[384,256]{1,0:T(8,128)(2,1)}, bf16[384,256]{1,0:T(8,128)(2,1)}) custom-call(bf16[384,5120]{1,0:T(8,128)(2,1)} %bitcast.6, bf16[5120,1280]{1,0:T(8,128)(2,1)} %wq_hbm.1, bf16[5120,256]{1,0:T(8,128)(2,1)} %wk_hbm.1, bf16[5120,256]{1,0:T(8,128)(2,1)} %wv_hbm.1, bf16[10,128]{1,0:T(8,128)(2,1)} %bitcast.9, ...), custom_call_target="tpu_custom_call" | custom-call | tf_op jit(solution)/shard_map/qkv_rope/pallas_call | solution.py:175
  17.5 24.5 %attend.1 = (bf16[3,128,1280]{2,1,0:T(8,128)(2,1)}, bf16[128,2,256,128]{3,2,1,0:T(8,128)(2,1)}, bf16[128,2,256,128]{3,2,1,0:T(8,128)(2,1)}) custom-call(s32[128]{0:T(128)} %len_ref.1, bf16[30,128,128]{2,1,0:T(8,128)(2,1)} %get-tuple-element.9.q_hbm, bf16[384,256]{1,0:T(8,128)(2,1)} %get-tuple-element.10.kn_hbm, bf16[384,256]{1,0:T(8,128)(2,1)} %get-tuple-element.11.vn_hbm, ...), custom_call_target="tpu_custom_call" | custom-call | tf_op jit(solution)/shard_map/attend/pallas_call | solution.py:321
  42.0 103.6 %wo_mlp.1 = bf16[3,128,5120]{2,1,0:T(8,128)(2,1)} custom-call(bf16[3,128,1280]{2,1,0:T(8,128)(2,1)} %get-tuple-element.12.o_hbm, bf16[3,128,5120]{2,1,0:T(8,128)(2,1)} %x_hbm.1, bf16[1280,5120]{1,0:T(8,128)(2,1)} %wo_hbm.1, bf16[5120,3456]{1,0:T(8,128)(2,1)} %w1_hbm.1, bf16[5120,3456]{1,0:T(8,128)(2,1)} %w3_hbm.1, bf16[3456,5120]{1,0:T(8,128)(2,1)} %w2_hbm.1, ...), custom_call_target="tpu_custom_call" | custom-call | tf_op jit(solution)/shard_map/wo_mlp/pallas_call | solution.py:720
  145.6 4.3 %copy.20 = bf16[3,128,5120]{2,1,0:T(8,128)(2,1)} copy(bf16[3,128,5120]{2,1,0:T(8,128)(2,1)} %wo_mlp.1) | data formatting | bytes 7864320

commit v4 on v3

--- a/solution.py
+++ b/solution.py
@@ -31,6 +31,13 @@
 VM = pl.BlockSpec(memory_space=pltpu.VMEM)
 SM = pl.BlockSpec(memory_space=pltpu.SMEM)
 HB = pl.BlockSpec(memory_space=pltpu.HBM)
+
+
+def loop(stop, body, start=0):
+    def step(i, carry):
+        body(i, carry)
+        return carry
+    lax.fori_loop(start, stop, step, 0)
 
 
 N_TILE = 512
@@ -307,9 +314,8 @@
                 o_buf[i % 2, t, :, hd * HEAD:(hd + 1) * HEAD] = slab.astype(BF16)
         for t in range(STEPS):
             o_copy(i, t).start()
-        return 0
-
-    lax.fori_loop(0, N_BLK, block, 0)
+
+    loop(N_BLK, block)
     for i in range(N_BLK - 2, N_BLK):
         for which in PAIR:
             out_copy(i, i % SLOTS, which).wait()
@@ -364,13 +370,14 @@
 WO_SLOTS = pl.cdiv(D_TILES, WO_PER)
 WO_AHEAD = 2
 B_LAG = 2
+NORM_ROWS = 32
 WHOLE = 2
 TAIL_ROWS = ((0, 2 * CHUNKS[1]), (2 * CHUNKS[1], CHUNKS[1]))
 
 
 def mlp_kernel(o_hbm, x_hbm, wo_hbm, w1_hbm, w3_hbm, w2_hbm, ga_hbm, gm_hbm,
                y_hbm,
-               o_v, xh0, xh1, u0, ps0, ps1, pr0, pr1, r10, r11, r20, r21, a0, a1, ring, ga_ref, gm_ref,
+               xh0, xh1, u0, ssq, ps0, ps1, pr0, pr1, r10, r11, r20, r21, a0, a1, ring, ga_ref, gm_ref, gain_f,
                in_sem, g_sem, wo_sem, ring_sem, res_sem, out_sem,
                p_send, p_recv, c_send, c_recv, a_send, a_recv, t_send, t_recv):
     me = lax.axis_index('tp')
@@ -384,7 +391,6 @@
     r_v = ((r10, r11), (r20, r21))
     a_v = (a0, a1)
     firsts = (0, CHUNKS[0])
-    row0 = (0, CROWS[0])
 
     barrier = pltpu.get_barrier_semaphore()
     for dev in (mate, peer):
@@ -444,7 +450,7 @@
         for t in range(STEPS):
             o_copies.append(pltpu.make_async_copy(
                 o_hbm.at[t, pl.ds(firsts[ch], CHUNKS[ch]), :],
-                o_v.at[pl.ds(row0[ch] + t * CHUNKS[ch], CHUNKS[ch]), :], in_sem.at[0, ch, t]))
+                xh[ch].at[pl.ds(t * CHUNKS[ch], CHUNKS[ch]), pl.ds(0, Q_W)], in_sem.at[0, ch, t]))
             x_copies.append(pltpu.make_async_copy(
                 x_hbm.at[t, pl.ds(firsts[ch], CHUNKS[ch]), :],
                 xh[ch].at[pl.ds(t * CHUNKS[ch], CHUNKS[ch]), :], in_sem.at[1, ch, t]))
@@ -504,36 +510,41 @@
         a_v[ch][own] = (a_v[ch][own].astype(F32) + r_v[ex][ch][k].astype(F32)).astype(BF16)
         gather_copy(ex, ch, k, core).start()
 
+    def sends_done(ex, ch):
+        def step(k, _):
+            gather_copy(ex, ch, k, core).wait_send()
+            mate_copy(ex, ch, k).wait_send()
+        loop(PIECES, step)
+
     def gather_done(ex, ch):
         def step(k, _):
-            gather_copy(ex, ch, k, core).wait_send()
             gather_copy(ex, ch, k, 1 - core).wait_recv()
-            mate_copy(ex, ch, k).wait_send()
-            return 0
-        lax.fori_loop(0, PIECES, step, 0)
+        loop(PIECES, step)
+        sends_done(ex, ch)
 
     def full_sums(ex, ch):
         def step(k, _):
             full_sum(ex, ch, k)
-            return 0
-        lax.fori_loop(0, PIECES, step, 0)
-
-    def norm_add(ch, gain_ref, then=None, steps=range(STEPS)):
+        loop(PIECES, step)
+
+    def norm_add(ch, which, then=None, steps=range(STEPS), squares=None):
         def step(b, _):
-            rows = pl.ds(pl.multiple_of(b * 16, 16), 16)
-            acc = jnp.zeros((16, PW), F32)
-            for j in range(D_TILES):
-                val = a_v[ch][j, rows, :].astype(F32)
-                acc = acc + val * val
+            rows = pl.ds(pl.multiple_of(b * NORM_ROWS, NORM_ROWS), NORM_ROWS)
+            if squares is None:
+                acc = jnp.zeros((NORM_ROWS, PW), F32)
+                for j in range(D_TILES):
+                    val = a_v[ch][j, rows, :].astype(F32)
+                    acc = acc + val * val
+            else:
+                acc = squares[rows, :]
             fac = lax.rsqrt(jnp.sum(acc, axis=1, keepdims=True) / float(D_MODEL) + NORM_EPS)
             for j in range(D_MODEL // HEAD):
                 cols = slice(j * HEAD, (j + 1) * HEAD)
                 val = a_v[ch][j * HEAD // PW, rows, j * HEAD % PW:j * HEAD % PW + HEAD].astype(F32)
                 base = xh[ch][rows, cols].astype(F32)
-                xh[ch][rows, cols] = (base + val * fac * gain_ref[j:j + 1, :].astype(F32)).astype(BF16)
-            return 0
+                xh[ch][rows, cols] = (base + val * fac * jnp.concatenate([gain_f[which, :, cols]] * (NORM_ROWS // 8))).astype(BF16)
         for t in steps:
-            lax.fori_loop(t * CHUNKS[ch] // 16, (t + 1) * CHUNKS[ch] // 16, step, 0)
+            loop((t + 1) * CHUNKS[ch] // NORM_ROWS, step, t * CHUNKS[ch] // NORM_ROWS)
             if then is not None:
                 then(t)
 
@@ -542,7 +553,7 @@
 
     def wo_tile(i, ch):
         rows = pl.ds(pl.multiple_of((i % WO_PER) * Q_W, Q_W), Q_W)
-        return jnp.dot(o_v[pl.ds(row0[ch], CROWS[ch]), :], ring[RING + i // WO_PER, rows, :],
+        return jnp.dot(xh[ch][:, pl.ds(0, Q_W)], ring[RING + i // WO_PER, rows, :],
                        preferred_element_type=F32).astype(BF16)
 
     def wo_sweep(ch):
@@ -562,14 +573,11 @@
             pair_sum(0, ch, k)
             if ch == 0:
                 peer_copy(0, ch, k).start()
-            return 0
-        lax.fori_loop(0, PIECES, step, 0)
+        loop(PIECES, step)
 
     pl.semaphore_wait(barrier, 2)
     with jax.named_scope('wo'):
         wo_sweep(0)
-        for cp in x_copies:
-            cp.start()
         for n in range(RING):
             stream(0, n, True)
         for r in range(WO_SLOTS, RESID):
@@ -577,26 +585,50 @@
                 cp.start()
         wo_sweep(1)
 
+    for cp in x_copies:
+        cp.start()
     for r in range(WO_SLOTS):
         for cp in res_copies(r):
             cp.start()
     with jax.named_scope('sums_a1'):
+        def add_squares(val):
+            for c in range(0, PW, HEAD):
+                part = val[:, c:c + HEAD]
+                ssq[...] = ssq[...] + part * part
+
+        def mate_square(k):
+            gather_copy(0, 0, k, 1 - core).wait_recv()
+            val = a_v[0][(1 - core) * HALF_T + k].astype(F32)
+            add_squares(val)
+
+        ssq[...] = jnp.zeros_like(ssq)
+        for which, gain_ref in enumerate((ga_ref, gm_ref)):
+            for j in range(D_MODEL // HEAD):
+                row = gain_ref[j:j + 1, :].astype(F32)
+                gain_f[which, :, j * HEAD:(j + 1) * HEAD] = jnp.broadcast_to(row, (8, HEAD))
+
         def first_sums(k, _):
             full_sum(0, 0, k)
+            val = a_v[0][core * HALF_T + k].astype(F32)
+            add_squares(val)
+
+            @pl.when(k >= 1)
+            def _():
+                mate_square(k - 1)
 
             @pl.when(k >= B_LAG)
             def _():
                 peer_copy(0, 1, k - B_LAG).start()
-            return 0
-        lax.fori_loop(0, PIECES, first_sums, 0)
+        loop(PIECES, first_sums)
         for k in range(PIECES - B_LAG, PIECES):
             peer_copy(0, 1, k).start()
     with jax.named_scope('gather_a1'):
-        gather_done(0, 0)
+        mate_square(PIECES - 1)
     for cp in x_copies:
         cp.wait()
     with jax.named_scope('norm_a1'):
-        norm_add(0, ga_ref)
+        norm_add(0, 0, squares=ssq)
+        sends_done(0, 0)
 
     def gate_up(ph, ch):
         def tile(i, slot):
@@ -608,7 +640,6 @@
         def single(q, _):
             tile(g_tile(q), stream(ph, q, False))
             refill(ph, q)
-            return 0
 
         def pair(q, _):
             slot = stream(ph, G_EXTRA + q, False)
@@ -618,9 +649,8 @@
             tile(2 * q, slot)
             tile(2 * q + 1, RING + q)
             refill(ph, G_EXTRA + q)
-            return 0
-        lax.fori_loop(0, G_EXTRA, single, 0)
-        lax.fori_loop(0, RESID, pair, 0)
+        loop(G_EXTRA, single)
+        loop(RESID, pair)
 
     def down(ph, ch, also, lag):
         def swap(k):
@@ -649,8 +679,7 @@
                 @pl.when(k < WHOLE)
                 def _():
                     peer_copy(1, ch, k).start()
-            return 0
-        lax.fori_loop(0, PIECES, step, 0)
+        loop(PIECES, step)
 
 
     with jax.named_scope('gate_up_a'):
@@ -660,7 +689,7 @@
     with jax.named_scope('gather_b1'):
         gather_done(0, 1)
     with jax.named_scope('norm_b1'):
-        norm_add(1, ga_ref)
+        norm_add(1, 0)
         pair_sum(1, 0, PIECES - 1)
         peer_copy(1, 0, PIECES - 1).start()
     with jax.named_scope('gate_up_b'):
@@ -678,12 +707,11 @@
     with jax.named_scope('gather_a2'):
         gather_done(1, 0)
     with jax.named_scope('norm_a2'):
-        norm_add(0, gm_ref, lambda t: y_copies(0)[t].start())
+        norm_add(0, 1, lambda t: y_copies(0)[t].start())
     with jax.named_scope('sums_b2'):
         def whole_sums(k, _):
             full_sum(1, 1, k)
-            return 0
-        lax.fori_loop(0, WHOLE, whole_sums, 0)
+        loop(WHOLE, whole_sums)
     for g in PAIR:
         rows = pl.ds(*TAIL_ROWS[g])
         with jax.named_scope(f'sums_b2#g={g}'):
@@ -697,18 +725,16 @@
                 def whole_done(k, _):
                     gather_copy(1, 1, k, core).wait_send()
                     gather_copy(1, 1, k, 1 - core).wait_recv()
-                    return 0
-                lax.fori_loop(0, WHOLE, whole_done, 0)
-
-                def sends_done(k, _):
+                loop(WHOLE, whole_done)
+
+                def mates_done(k, _):
                     mate_copy(1, 1, k).wait_send()
-                    return 0
-                lax.fori_loop(0, PIECES, sends_done, 0)
+                loop(PIECES, mates_done)
             for k in range(WHOLE, PIECES):
                 tail_gather(g, k, core).wait_send()
                 tail_gather(g, k, 1 - core).wait_recv()
         with jax.named_scope(f'norm_b2#g={g}'):
-            norm_add(1, gm_ref, lambda t: y_copies(1)[t].start(), ((0, 1), (2,))[g])
+            norm_add(1, 1, lambda t: y_copies(1)[t].start(), ((0, 1), (2,))[g])
     with jax.named_scope('y_out'):
         for ch in PAIR:
             for cp in y_copies(ch):
@@ -723,13 +749,14 @@
         in_specs=[HB] * 8,
         out_specs=HB,
         scratch_shapes=[
-            pltpu.VMEM((ROWS, Q_W), BF16),
             *[pltpu.VMEM((n, D_MODEL), BF16) for n in CROWS],
             pltpu.VMEM((max(CROWS), FF_LOC), BF16),
+            pltpu.VMEM((CROWS[0], HEAD), F32),
             *[pltpu.VMEM((PIECES, n, PW), BF16) for n in CROWS * 4],
             *[pltpu.VMEM((D_TILES, n, PW), BF16) for n in CROWS],
             pltpu.VMEM((RING + RESID, D_MODEL, PW), BF16),
             *[pltpu.VMEM((D_MODEL // HEAD, HEAD), BF16)] * 2,
+            pltpu.VMEM((2, 8, D_MODEL), F32),
             sem((2, 2, STEPS)), sem((2,)), sem((D_TILES,)), sem((RING, 2)), sem((RESID, 2)), sem((2, STEPS)),
             *[sem((2, 2, PIECES))] * 6,
             *[sem((2, 2, PIECES - WHOLE))] * 2,
@@ -749,10 +776,10 @@
         y = run_mlp(o, x_seq, w_o, w_gate, w_up, w_down, tiled(g_attn), tiled(g_mlp))
         return y, k_out, v_out
 
-    data_spec = P(None, 'dp', None)
-    cache_spec = P('dp', 'tp', None, None)
+    data_spec = P(None, 'dp')
+    cache_spec = P('dp', 'tp')
     col_spec = P(None, 'tp')
-    row_spec = P('tp', None)
-    arg_specs = (data_spec, P('dp'), cache_spec, cache_spec, col_spec, col_spec, col_spec, row_spec, col_spec, col_spec, row_spec, P('tp'), P('tp'), P(None), P(None))
+    row_spec = P('tp')
+    arg_specs = (data_spec, P('dp'), cache_spec, cache_spec, col_spec, col_spec, col_spec, row_spec, col_spec, col_spec, row_spec, P('tp'), P('tp'), P(), P())
     out_specs = (data_spec, cache_spec, cache_spec)
     return jax.shard_map(local_run, mesh=mesh, in_specs=arg_specs, out_specs=out_specs, check_vma=False)

time: 150 us -> 149 us (level)
  Pallas kernels: 145 us -> 143 us
    pallas_call x1, Pallas kernels: 104 us -> 102 us  [run_mlp(): pl.pallas_call(mlp_kernel, out_shape=jax.ShapeDtypeStruct((STEPS, BATCH,...]
where the time goes in v4:
time: 149 us; the launch traced here: 148 us
  Pallas kernels  143 us (96%)
  local copies, waits for them, and re-layouts  4.29 us (3%)
    pallas_call x1, Pallas kernels, run_mlp(): pl.pallas_call(mlp_kernel, out_shape=jax.ShapeDtypeStruct((STEPS, BATCH,...  102 us
    pallas_call x1, Pallas kernels, run_attn(): pl.pallas_call(attn_kernel, out_shape=(jax.ShapeDtypeStruct((STEPS, BATCH...  24.4 us
    pallas_call x1, Pallas kernels, run_qkv(): pl.pallas_call(qkv_kernel, out_shape=(jax.ShapeDtypeStruct((30, BATCH, HE...  16.9 us
    unnamed x1, local copies, waits for them, and re-layouts  4.29 us

profile of v4, /device:TPU:0, one launch (start us, length us, event | category | flops | bytes accessed | tf_op | source)
XLA Modules:
  0.0 148.3 jit_solution(10703519940785129470)
XLA Ops:
  0.6 16.9 %qkv_rope.1 = (bf16[30,128,128]{2,1,0:T(8,128)(2,1)}, bf16[384,256]{1,0:T(8,128)(2,1)}, bf16[384,256]{1,0:T(8,128)(2,1)}) custom-call(bf16[384,5120]{1,0:T(8,128)(2,1)} %bitcast.6, bf16[5120,1280]{1,0:T(8,128)(2,1)} %wq_hbm.1, bf16[5120,256]{1,0:T(8,128)(2,1)} %wk_hbm.1, bf16[5120,256]{1,0:T(8,128)(2,1)} %wv_hbm.1, bf16[10,128]{1,0:T(8,128)(2,1)} %bitcast.9, ...), custom_call_target="tpu_custom_call" | custom-call | tf_op jit(solution)/shard_map/qkv_rope/pallas_call | solution.py:182
  17.5 24.4 %attend.1 = (bf16[3,128,1280]{2,1,0:T(8,128)(2,1)}, bf16[128,2,256,128]{3,2,1,0:T(8,128)(2,1)}, bf16[128,2,256,128]{3,2,1,0:T(8,128)(2,1)}) custom-call(s32[128]{0:T(128)} %len_ref.1, bf16[30,128,128]{2,1,0:T(8,128)(2,1)} %get-tuple-element.9.q_hbm, bf16[384,256]{1,0:T(8,128)(2,1)} %get-tuple-element.10.kn_hbm, bf16[384,256]{1,0:T(8,128)(2,1)} %get-tuple-element.11.vn_hbm, ...), custom_call_target="tpu_custom_call" | custom-call | tf_op jit(solution)/shard_map/attend/pallas_call | solution.py:327
  42.0 102.0 %wo_mlp.1 = bf16[3,128,5120]{2,1,0:T(8,128)(2,1)} custom-call(bf16[3,128,1280]{2,1,0:T(8,128)(2,1)} %get-tuple-element.12.o_hbm, bf16[3,128,5120]{2,1,0:T(8,128)(2,1)} %x_hbm.1, bf16[1280,5120]{1,0:T(8,128)(2,1)} %wo_hbm.1, bf16[5120,3456]{1,0:T(8,128)(2,1)} %w1_hbm.1, bf16[5120,3456]{1,0:T(8,128)(2,1)} %w3_hbm.1, bf16[3456,5120]{1,0:T(8,128)(2,1)} %w2_hbm.1, ...), custom_call_target="tpu_custom_call" | custom-call | tf_op jit(solution)/shard_map/wo_mlp/pallas_call | solution.py:746
  144.0 4.3 %copy.20 = bf16[3,128,5120]{2,1,0:T(8,128)(2,1)} copy(bf16[3,128,5120]{2,1,0:T(8,128)(2,1)} %wo_mlp.1) | data formatting | bytes 7864320

commit v5 on v4

--- a/solution.py
+++ b/solution.py
@@ -766,6 +766,35 @@
     )(o, x_seq, w_o, w_gate, w_up, w_down, g_a, g_m)
 
 
+Y_ROWS = 32
+
+
+def copy_kernel(y_in, y_out, buf, in_sem, out_sem):
+    pieces = [(t, pl.ds(r, Y_ROWS)) for t in range(STEPS) for r in range(0, BATCH, Y_ROWS)]
+    ins = [pltpu.make_async_copy(y_in.at[p], buf.at[p], in_sem.at[n]) for n, p in enumerate(pieces)]
+    outs = [pltpu.make_async_copy(buf.at[p], y_out.at[p], out_sem.at[n]) for n, p in enumerate(pieces)]
+    for cp in ins:
+        cp.start()
+    for came, goes in zip(ins, outs):
+        came.wait()
+        goes.start()
+    for cp in outs:
+        cp.wait()
+
+
+def run_copy(y):
+    n = STEPS * BATCH // Y_ROWS
+    return pl.pallas_call(
+        copy_kernel,
+        out_shape=jax.ShapeDtypeStruct(y.shape, BF16),
+        in_specs=[HB],
+        out_specs=HB,
+        scratch_shapes=[pltpu.VMEM(y.shape, BF16), *[pltpu.SemaphoreType.DMA((n,))] * 2],
+        compiler_params=pltpu.CompilerParams(vmem_limit_bytes=VMEM_ALL),
+        name='place_y',
+    )(y)
+
+
 def solution(mesh):
     def local_run(x_seq, cache_len, k_cache, v_cache, w_q, w_k, w_v, w_o, w_gate, w_up, w_down, g_q, g_k, g_attn, g_mlp):
         inv_freq = ROPE_THETA ** (-(np.arange(HEAD // 2, dtype=np.float32) * np.float32(2.0 / HEAD)))
@@ -774,7 +803,7 @@
         q_rot, k_new, v_new = run_qkv(x_seq.reshape(ROWS, D_MODEL), w_q, w_k, w_v, tiled(g_q), tiled(g_k), cache_len[None, :], freq_row)
         o, k_out, v_out = run_attn(cache_len, q_rot, k_new, v_new, k_cache, v_cache)
         y = run_mlp(o, x_seq, w_o, w_gate, w_up, w_down, tiled(g_attn), tiled(g_mlp))
-        return y, k_out, v_out
+        return run_copy(y), k_out, v_out
 
     data_spec = P(None, 'dp')
     cache_spec = P('dp', 'tp')

time: 149 us -> 148 us (level)
  local copies, waits for them, and re-layouts: 4.29 us -> 0 us
  Pallas kernels: 143 us -> 147 us
    unnamed x1 -> x0, local copies, waits for them, and re-layouts: 4.29 us -> none
    pallas_call x0 -> x1, Pallas kernels: none -> 3.47 us  [run_copy(): pl.pallas_call(copy_kernel, out_shape=jax.ShapeDtypeStruct(y.shape, BF16)...]
where the time goes in v5:
time: 148 us
  Pallas kernels  147 us (99%)
    pallas_call x1, Pallas kernels, run_mlp(): pl.pallas_call(mlp_kernel, out_shape=jax.ShapeDtypeStruct((STEPS, BATCH,...  102 us
    pallas_call x1, Pallas kernels, run_attn(): pl.pallas_call(attn_kernel, out_shape=(jax.ShapeDtypeStruct((STEPS, BATCH...  24.5 us
    pallas_call x1, Pallas kernels, run_qkv(): pl.pallas_call(qkv_kernel, out_shape=(jax.ShapeDtypeStruct((30, BATCH, HE...  16.9 us
    pallas_call x1, Pallas kernels, run_copy(): pl.pallas_call(copy_kernel, out_shape=jax.ShapeDtypeStruct(y.shape, BF16)...  3.47 us

profile of v5, /device:TPU:0, one launch (start us, length us, event | category | flops | bytes accessed | tf_op | source)
XLA Modules:
  0.0 147.7 jit_solution(7799478282237202569)
XLA Ops:
  0.6 16.9 %qkv_rope.1 = (bf16[30,128,128]{2,1,0:T(8,128)(2,1)}, bf16[384,256]{1,0:T(8,128)(2,1)}, bf16[384,256]{1,0:T(8,128)(2,1)}) custom-call(bf16[384,5120]{1,0:T(8,128)(2,1)} %bitcast.6, bf16[5120,1280]{1,0:T(8,128)(2,1)} %wq_hbm.1, bf16[5120,256]{1,0:T(8,128)(2,1)} %wk_hbm.1, bf16[5120,256]{1,0:T(8,128)(2,1)} %wv_hbm.1, bf16[10,128]{1,0:T(8,128)(2,1)} %bitcast.9, ...), custom_call_target="tpu_custom_call" | custom-call | tf_op jit(solution)/shard_map/qkv_rope/pallas_call | solution.py:182
  17.5 24.5 %attend.1 = (bf16[3,128,1280]{2,1,0:T(8,128)(2,1)}, bf16[128,2,256,128]{3,2,1,0:T(8,128)(2,1)}, bf16[128,2,256,128]{3,2,1,0:T(8,128)(2,1)}) custom-call(s32[128]{0:T(128)} %len_ref.1, bf16[30,128,128]{2,1,0:T(8,128)(2,1)} %get-tuple-element.9.q_hbm, bf16[384,256]{1,0:T(8,128)(2,1)} %get-tuple-element.10.kn_hbm, bf16[384,256]{1,0:T(8,128)(2,1)} %get-tuple-element.11.vn_hbm, ...), custom_call_target="tpu_custom_call" | custom-call | tf_op jit(solution)/shard_map/attend/pallas_call | solution.py:327
  42.0 102.0 %wo_mlp.1.y_in = bf16[3,128,5120]{2,1,0:T(8,128)(2,1)} custom-call(bf16[3,128,1280]{2,1,0:T(8,128)(2,1)} %get-tuple-element.12.o_hbm, bf16[3,128,5120]{2,1,0:T(8,128)(2,1)} %x_hbm.1, bf16[1280,5120]{1,0:T(8,128)(2,1)} %wo_hbm.1, bf16[5120,3456]{1,0:T(8,128)(2,1)} %w1_hbm.1, bf16[5120,3456]{1,0:T(8,128)(2,1)} %w3_hbm.1, bf16[3456,5120]{1,0:T(8,128)(2,1)} %w2_hbm.1, ...), custom_call_target="tpu_custom_call" | custom-call | tf_op jit(solution)/shard_map/wo_mlp/pallas_call | solution.py:746
  144.1 3.5 %place_y.1 = bf16[3,128,5120]{2,1,0:T(8,128)(2,1)} custom-call(bf16[3,128,5120]{2,1,0:T(8,128)(2,1)} %wo_mlp.1.y_in), custom_call_target="tpu_custom_call" | custom-call | tf_op jit(solution)/shard_map/place_y/pallas_call | solution.py:787
